TPU v7x, 32 devices: a whole 2x2x4 slice. The times are simulated.
32 devices in a mesh: expert: 16 (over z, y, core), replica: 2 (over x).
Axes of the slice: x: 2, y: 2, z: 4, core: 2. Of those that a mesh axis runs over, the one named last changes fastest.
Arguments:
- tokens: bfloat16 [4096, 2048], P(('expert', 'replica')), may hold values from -15 to 15
- cotangents: bfloat16 [4096, 768], P(('expert', 'replica')), may hold values from -6 to 6
- routes: int32 [4096, 8], P(('expert', 'replica')), may hold values from 0 to 127, all different within a row; in each aligned block of 128 rows (0 to 127, 128 to 255, ...) at most 12 rows name the same one
- owner: int32 [16], P('expert'), may hold values from 0 to 1
- a_inverse: bfloat16 [16, 2048, 2048], P('expert', 'replica'), may hold values from -1 to 33, as said below
- g_inverse: bfloat16 [16, 768, 768], P('expert'), may hold values from -1 to 33
Outputs:
- a_factor: float32 [16, 2048, 2048], P('expert', 'replica')
- kept_factor: float32 [2, 16, 768, 768], P('replica', 'expert')
- update: bfloat16 [16, 2048, 768], P('expert')
Inputs may be any that keep to these rules, and one draw needn't show every extreme that they name: `routes`: the 8 ids of a row differ; among the rows of one device no id occurs more than 12 times and some id occurs exactly 12 times; every id occurs somewhere. Each a_inverse[v] is symmetric.
All inputs are finite; a program needn't handle non-finite values.
Results may differ from a plain program's by a relative error of at most 0.018.
Values may be sent and summed in bfloat16 or wider, within the bound.
No kernel may reach another device: no remote copies, remote signals or barrier semaphores. Data moves between devices by JAX's collectives and lax.ppermute only.
A program may use at most 128 MiB of HBM per device.

v0:
```python
import jax
import jax.numpy as jnp
from jax import lax
from jax.sharding import PartitionSpec as P

CAP = 12


def slot_table(route_block, expert_count, capacity):
    top_k = route_block.shape[1]
    route_ids = route_block.reshape(-1)
    in_window = route_ids < expert_count
    columns = lax.broadcasted_iota(jnp.int32, (route_ids.shape[0], expert_count), 1)
    one_hot = ((route_ids[:, None] == columns) & in_window[:, None]).astype(jnp.int32)
    before = jnp.cumsum(one_hot, axis=0) - one_hot
    position = jnp.sum(before * one_hot, axis=1)
    sentinel = expert_count * capacity
    slot_ids = jnp.where(in_window, route_ids * capacity + position, sentinel)
    source_ids = jnp.arange(route_ids.shape[0], dtype=jnp.int32) // top_k
    slot_token = jnp.zeros((sentinel + 1,), jnp.int32).at[slot_ids].set(source_ids)
    filled = jnp.zeros((sentinel + 1,), jnp.int32).at[slot_ids].set(1)
    return (slot_token[:sentinel], filled[:sentinel])


def local(tokens, cotangents, routes, owner, a_inverse, g_inverse):
    expert_count = lax.axis_size("expert")
    replica_count = lax.axis_size("replica")
    width = tokens.shape[1]
    hidden_width = cotangents.shape[1]
    slot_token, filled = slot_table(routes, expert_count, CAP)
    slot_mask = filled.astype(jnp.bfloat16)[:, None]
    send_x = (jnp.take(tokens, slot_token, axis=0) * slot_mask).reshape(expert_count, CAP, width)
    send_y = (jnp.take(cotangents, slot_token, axis=0) * slot_mask).reshape(
        expert_count, CAP, hidden_width
    )
    sent_counts = jnp.sum(filled.reshape(expert_count, CAP), axis=1).astype(jnp.bfloat16)
    recv_x, recv_y, recv_counts = (
        lax.all_to_all(send_x, "expert", split_axis=0, concat_axis=0, tiled=True),
        lax.all_to_all(send_y, "expert", split_axis=0, concat_axis=0, tiled=True),
        lax.all_to_all(sent_counts, "expert", split_axis=0, concat_axis=0, tiled=True),
    )
    rows_x = recv_x.reshape(-1, width)
    rows_y = recv_y.reshape(-1, hidden_width)
    block_rows = width // replica_count
    shard_rows = rows_x.shape[0]
    own_start = lax.axis_index("replica") * block_rows
    piece_x = lax.all_gather(rows_x, "replica", axis=0, tiled=True)
    piece_y = lax.all_gather(rows_y, "replica", axis=0, tiled=True)
    piece_counts = lax.all_gather(recv_counts, "replica", axis=0, tiled=True)
    shards = piece_x.shape[0] // shard_rows
    columns = lax.dynamic_slice_in_dim(piece_x, own_start, block_rows, 1)
    a_next = jnp.dot(columns.T, piece_x, preferred_element_type=jnp.float32)
    split_cols = columns.reshape(shards, shard_rows, block_rows)
    split_y = piece_y.reshape(shards, shard_rows, hidden_width)
    w_parts = jnp.einsum(
        "snd,snh->sdh", split_cols, split_y, preferred_element_type=jnp.float32
    ).astype(jnp.bfloat16)
    w_parts = lax.optimization_barrier(w_parts).astype(jnp.float32)
    g_parts = jnp.einsum(
        "snh,sng->shg", split_y, split_y, preferred_element_type=jnp.float32
    ).astype(jnp.bfloat16)
    g_parts = lax.optimization_barrier(g_parts).astype(jnp.float32)
    grad_next = jnp.sum(w_parts, axis=0)
    g_next = jnp.sum(g_parts, axis=0)
    count_next = jnp.sum(piece_counts.astype(jnp.float32))
    grad_local = (grad_next / count_next).astype(jnp.bfloat16)
    a_local = a_inverse[0]
    columns = a_local
    mixed = lax.psum_scatter(
        jnp.dot(columns.T, grad_local, preferred_element_type=jnp.float32).astype(jnp.bfloat16),
        "replica",
        scatter_dimension=0,
        tiled=True,
    )
    update_local = jnp.dot(mixed, g_inverse[0], preferred_element_type=jnp.float32).astype(
        jnp.bfloat16
    )
    update = lax.all_gather(update_local, "replica", axis=0, tiled=True)
    a_factor = (a_next / count_next)[None]
    keeper = owner[0] == lax.axis_index("replica")
    kept = jnp.where(keeper, g_next / count_next, jnp.zeros_like(g_next))[None, None]
    return (a_factor, kept, update[None])


def solution(mesh):
    placed = (
        P(("expert", "replica"), None),
        P(("expert", "replica"), None),
        P(("expert", "replica"), None),
        P("expert"),
        P("expert", "replica", None),
        P("expert", None, None),
    )
    return jax.shard_map(
        local,
        mesh=mesh,
        in_specs=placed,
        out_specs=(
            P("expert", "replica", None),
            P("replica", "expert", None, None),
            P("expert", None, None),
        ),
        check_vma=False,
    )
```

profile of v0, /device:TPU:0, one launch (start us, length us, event | category | flops | bytes accessed | tf_op | source)
XLA Modules:
  0.0 208.2 jit_solution(11059449409683475876)
XLA Ops:
  7.2 0.8 broadcast_compare_fusion.2
  8.1 0.7 broadcast_multiply_fusion
  8.8 0.8 copy.26
  9.5 0.1 eq.24
  9.6 0.1 eq.21
  9.7 0.1 copy.24
  9.9 0.1 lt.61
  10.0 0.1 copy.25
  10.1 0.1 mul.42
  10.2 4.5 %reduce-window.6 = s32[16,8,128]{2,1,0:T(8,128)S(1)} reduce-window(s32[16,8,128]{2,1,0:T(8,128)S(1)} %fusion.15, s32[]{:T(128)} %constant.35.clone.1), window={size=1x1x128 pad=0_0x0_0x127_0}, to_apply=%region_0.0 | reduce-window | flops 2080768 | bytes 131076 | tf_op jit(solution)/shard_map/reduce-window
  14.8 0.1 copy.28
  15.0 0.1 broadcast_add_fusion
  15.2 4.3 %scatter_custom_fusion.1 = s32[193]{0:T(256)S(1)} fusion(s32[1024]{0:T(1024)S(1)} %bitcast.61, s32[1024]{0:T(1024)S(1)} %ne.14, s32[]{:T(128)} %constant.35.clone.1), kind=kCustom, calls=%fused_computation.48 | custom fusion | bytes 776 | tf_op jit(solution)/shard_map/scatter | solution.py:21
  19.5 4.3 %scatter_custom_fusion = s32[193]{0:T(256)S(1)} fusion(s32[1024]{0:T(1024)S(1)} %bitcast.62, s32[1024]{0:T(1024)S(1)} %add_select_fusion, s32[]{:T(128)} %constant.35.clone.1), kind=kCustom, calls=%fused_computation.50 | custom fusion | bytes 776 | tf_op jit(solution)/shard_map/scatter | solution.py:20
  23.9 0.1 slice.19
  24.0 0.1 fusion.23
  24.2 1.1 gather_fusion
  25.3 0.2 gather.13
  25.5 0.2 select_multiply_fusion
  25.7 32.0 %all_to_all.19 = bf16[16,12,2048]{2,1,0:T(8,128)(2,1)S(1)} all-to-all(bf16[16,12,2048]{2,1,0:T(8,128)(2,1)S(1)} %select_multiply_fusion), channel_id=1, replica_groups=mesh['expert'=16,'replica'=2] {'expert'}, dimensions={0} | all-to-all | bytes 1572864 | tf_op jit(solution)/shard_map/all_to_all | solution.py:38
  57.7 1.1 reshape.142
  58.8 0.7 copy.30
  59.5 5.0 %all-to-all-start.1 = ((bf16[16,1,1]{2,1,0:T(2,128)(2,1)}), bf16[16,1,1]{2,1,0:T(2,128)(2,1)S(1)}, u32[]{:S(2)}, u32[]{:S(2)}) async-start(bf16[16,1,1]{2,1,0:T(2,128)(2,1)} %copy.30), calls=%async_computation.1 | async-start | bytes 16384 | tf_op jit(solution)/shard_map/all_to_all | solution.py:40
  64.6 1.0 gather_fusion.1
  65.7 0.9 select_multiply_fusion.1
  66.6 4.3 %all-to-all-done.1 = bf16[16,1,1]{2,1,0:T(2,128)(2,1)S(1)} async-done(((bf16[16,1,1]{2,1,0:T(2,128)(2,1)}), bf16[16,1,1]{2,1,0:T(2,128)(2,1)S(1)}, u32[]{:S(2)}, u32[]{:S(2)}) %all-to-all-start.1) | async-done | bytes 64 | tf_op jit(solution)/shard_map/all_to_all | solution.py:40
  70.9 3.6 %all-to-all-start.2 = ((bf16[16,12,768]{2,1,0:T(8,128)(2,1)}), bf16[16,12,768]{2,1,0:T(8,128)(2,1)S(1)}, u32[]{:S(2)}, u32[]{:S(2)}) async-start(bf16[16,12,768]{2,1,0:T(8,128)(2,1)} %select_multiply_fusion.1), calls=%async_computation.2 | async-start | bytes 786432 | tf_op jit(solution)/shard_map/all_to_all | solution.py:39
  74.5 0.6 dynamic-slice
  75.8 0.2 reduce.2
  76.0 0.2 dynamic-update-slice
  76.2 5.1 %all-reduce = bf16[32]{0:T(256)(128)(2,1)S(1)} all-reduce(bf16[32]{0:T(256)(128)(2,1)S(1)} %dynamic-update-slice), channel_id=2, replica_groups=mesh['expert'=16,'replica'=2] {'replica'}, use_global_device_ids=true, to_apply=%add | all-reduce | flops 32 | bytes 128
  81.3 0.6 convert_reduce_fusion.2
  81.9 4.7 %all-to-all-done.2 = bf16[16,12,768]{2,1,0:T(8,128)(2,1)S(1)} async-done(((bf16[16,12,768]{2,1,0:T(8,128)(2,1)}), bf16[16,12,768]{2,1,0:T(8,128)(2,1)S(1)}, u32[]{:S(2)}, u32[]{:S(2)}) %all-to-all-start.2) | async-done | bytes 294944 | tf_op jit(solution)/shard_map/all_to_all | solution.py:39
  86.7 9.7 %all_gather.14 = bf16[384,768]{1,0:T(8,128)(2,1)S(1)} all-gather(bf16[192,768]{1,0:T(8,128)(2,1)S(1)} %reshape.143), channel_id=1, replica_groups=mesh['expert'=16,'replica'=2] {'replica'}, dimensions={0}, use_global_device_ids=true | all-gather | bytes 884736 | tf_op jit(solution)/shard_map/all_gather | solution.py:48
  96.4 1.2 constant_dynamic-slice_fusion
  97.5 1.1 convolution_convert_fusion
  98.6 0.5 convert_reduce_fusion
  99.2 1.6 copy-done.4
  100.8 5.5 %fusion.5 = bf16[2048,768]{0,1:T(8,128)(2,1)} fusion(bf16[1,1024,2048]{2,1,0:T(8,128)(2,1)S(1)} %copy-done.4, f32[1024,768]{1,0:T(8,128)S(1)} %convert_reduce_fusion, f32[]{:T(128)} %convert_reduce_fusion.2), kind=kOutput, calls=%fused_computation.11 | convolution fusion | flops 3224371200 | bytes 10485764 | tf_op jit(solution)/shard_map/dot_general | solution.py:70
  106.3 0.2 all-gather.6.cloned.1.call-start
  106.5 42.3 %reduce-scatter.2.cloned.1.call-done = bf16[1024,768]{0,1:T(8,128)(2,1)} async-done(((bf16[2048,768]{0,1:T(8,128)(2,1)}), bf16[1024,768]{0,1:T(8,128)(2,1)}) %reduce-scatter.2.cloned.1.call-update) | async-done | bytes 1572880 | tf_op jit(solution)/shard_map/reduce_scatter | solution.py:69
  148.8 4.0 %convolution_convert_fusion.2 = bf16[1024,768]{1,0:T(8,128)(2,1)} fusion(bf16[1024,768]{0,1:T(8,128)(2,1)} %reduce-scatter.2.cloned.1.call-done, bf16[1,768,768]{2,1,0:T(8,128)(2,1)S(1)} %copy-done), kind=kOutput, calls=%fused_computation.15 | convolution fusion | flops 1208745984 | bytes 4325376 | tf_op jit(solution)/shard_map/dot_general | solution.py:75
  153.5 0.9 convolution_convert_fusion.1
  154.4 0.4 convert_reduce_fusion.1
  154.8 2.2 %select_bitcast_fusion = f32[1,1,768,768]{3,2,1,0:T(8,128)} fusion(f32[768,768]{1,0:T(8,128)S(1)} %convert_reduce_fusion.1, f32[]{:T(128)} %convert_reduce_fusion.2, pred[]{:T(512)S(6)} %eq.27), kind=kLoop, calls=%fused_computation.12 | loop fusion | flops 1179648 | bytes 4718597 | tf_op jit(solution)/shard_map/jit(_where)/select_n | solution.py:81
  157.0 6.6 %divide_bitcast_fusion = f32[1,1024,2048]{2,1,0:T(8,128)} fusion(f32[]{:T(128)} %convert_reduce_fusion.2, bf16[384,1024]{1,0:T(8,128)(2,1)S(1)} %constant_dynamic-slice_fusion, bf16[384,2048]{1,0:T(8,128)(2,1)S(1)} %copy-done.3), kind=kOutput, calls=%fused_computation.4 | convolution fusion | flops 1612709888 | bytes 10747908 | tf_op jit(solution)/shard_map/dot_general | solution.py:52
  163.6 34.3 %all-gather.6.cloned.1.call-done = bf16[2048,768]{1,0:T(8,128)(2,1)} async-done(((bf16[1024,768]{1,0:T(8,128)(2,1)}), bf16[2048,768]{1,0:T(8,128)(2,1)}) %all-gather.6.cloned.1.call-update) | async-done | bytes 3145744 | tf_op jit(solution)/shard_map/all_gather | solution.py:78
  197.9 3.8 %copy.36 = bf16[1,2048,768]{2,1,0:T(8,128)(2,1)} copy(bf16[1,2048,768]{2,1,0:T(8,128)(2,1)} %bitcast.56) | data formatting | bytes 6291456
  (36 shorter events, 0.7 us)
Async XLA Ops:
  7.2 141.7 %copy-start = (bf16[1,768,768]{2,1,0:T(8,128)(2,1)S(1)}, bf16[1,768,768]{2,1,0:T(8,128)(2,1)}, u32[]{:S(2)}) copy-start(bf16[1,768,768]{2,1,0:T(8,128)(2,1)} %param.11) | copy-start | bytes 3538948
  7.2 17.0 %copy-start.1 = (bf16[128,2048]{1,0:T(8,128)(2,1)S(1)}, bf16[128,2048]{1,0:T(8,128)(2,1)}, u32[]{:S(2)}) copy-start(bf16[128,2048]{1,0:T(8,128)(2,1)} %param.6) | copy-start | bytes 1572868
  7.2 89.2 %all-gather.4.cloned.1.call-start = ((), (), s32[]{:S(2)}) async-start(), calls=%async_computation.4 | async-start | bytes 2359296 | tf_op jit(solution)/shard_map/all_gather | solution.py:47
  25.7 38.9 %copy-start.2 = (bf16[128,768]{1,0:T(8,128)(2,1)S(1)}, bf16[128,768]{1,0:T(8,128)(2,1)}, u32[]{:S(2)}) copy-start(bf16[128,768]{1,0:T(8,128)(2,1)} %param.7) | copy-start | bytes 589828
  59.5 11.4 %all-to-all-start.1 = ((bf16[16,1,1]{2,1,0:T(2,128)(2,1)}), bf16[16,1,1]{2,1,0:T(2,128)(2,1)S(1)}, u32[]{:S(2)}, u32[]{:S(2)}) async-start(bf16[16,1,1]{2,1,0:T(2,128)(2,1)} %copy.30), calls=%async_computation.1 | async-start | bytes 16384 | tf_op jit(solution)/shard_map/all_to_all | solution.py:40
  64.5 10.0 %copy-start.5 = (u32[32]{0:T(128)S(1)}, u32[32]{0:T(128)}, u32[]{:S(2)}) copy-start(u32[32]{0:T(128)} %constant.77) | copy-start | bytes 388
  70.9 15.7 %all-to-all-start.2 = ((bf16[16,12,768]{2,1,0:T(8,128)(2,1)}), bf16[16,12,768]{2,1,0:T(8,128)(2,1)S(1)}, u32[]{:S(2)}, u32[]{:S(2)}) async-start(bf16[16,12,768]{2,1,0:T(8,128)(2,1)} %select_multiply_fusion.1), calls=%async_computation.2 | async-start | bytes 786432 | tf_op jit(solution)/shard_map/all_to_all | solution.py:39
  74.5 74.4 %reduce-scatter.2.cloned.1.call-start = ((), (), s32[]{:S(2)}) async-start(), calls=%async_computation.5 | async-start | bytes 4718592 | tf_op jit(solution)/shard_map/reduce_scatter | solution.py:69
  98.6 2.2 %copy-start.4 = (bf16[1,1024,2048]{2,1,0:T(8,128)(2,1)S(1)}, bf16[1,1024,2048]{2,1,0:T(8,128)(2,1)}, u32[]{:S(2)}) copy-start(bf16[1,1024,2048]{2,1,0:T(8,128)(2,1)} %param.10) | copy-start | bytes 12582916
  106.3 91.6 %all-gather.6.cloned.1.call-start = ((), (), s32[]{:S(2)}) async-start(), calls=%async_computation.6 | async-start | bytes 4718592 | tf_op jit(solution)/shard_map/all_gather | solution.py:78
  154.8 2.2 %copy-start.3 = (bf16[384,2048]{1,0:T(8,128)(2,1)S(1)}, bf16[384,2048]{1,0:T(8,128)(2,1)}, u32[]{:S(2)}) copy-start(bf16[384,2048]{1,0:T(8,128)(2,1)} %all-gather.4.cloned.1.call-done) | copy-start | bytes 4718596
Sparse Core Ops, SparseCore 0:
  58.9 27.6 all-gather.3
  106.4 42.3 reduce-scatter.1
  153.0 44.8 all-gather.5
where the time goes:
time: 209 us; the launch traced here: 208 us
  waiting for transfers between devices  85.7 us (41%)
  blocking collectives  46.8 us (22%)
  local copies, waits for them, and re-layouts  22.1 us (11%)
  matrix products  18 us (9%)
  between operations  15.3 us (7%)
  other arithmetic  11.4 us (5%)
  starting transfers between devices  8.88 us (4%)
    reduce_scatter x1, waiting for transfers between devices, local(): lax.psum_scatter(jnp.dot(columns.T, grad_local, preferred_element_type=jn...  42.3 us
    all_gather x1, waiting for transfers between devices, local(): update = lax.all_gather(update_local, 'replica', axis=0, tiled=True)  34.3 us
    all_to_all x1, blocking collectives, local(): lax.all_to_all(send_x, 'expert', split_axis=0, concat_axis=0, tiled=True)  32 us
    all_gather x1, blocking collectives, local(): piece_y = lax.all_gather(rows_y, 'replica', axis=0, tiled=True)  9.69 us
    unnamed x17, local copies, waits for them, and re-layouts  7.03 us
    dot_general x1, matrix products, local(): a_next = jnp.dot(columns.T, piece_x, preferred_element_type=jnp.float32)  6.59 us
    dot_general x1, matrix products, local(): jnp.dot(columns.T, grad_local, preferred_element_type=jnp.float32)  5.48 us
    unnamed x1, blocking collectives  5.12 us
  transfers between devices with their start and end apart: 5, of which 4 were waited for; matrix products, arithmetic and copies ran while one was open for 7% of the time, Pallas kernels for 0%

commit v1 on v0

v1 whole, which is shorter than its diff:
```python
import functools

import jax
import jax.numpy as jnp
from jax import lax
from jax.experimental import pallas as pl
from jax.experimental.pallas import tpu as pltpu
from jax.sharding import PartitionSpec as P


CAP = 12
MAIN = 8
EMPTY = 1024.0

PAD = 16
TILE = 256
RING = 4
AHEAD = 256


F32 = jnp.float32
BF16 = jnp.bfloat16
VMEM = pl.BlockSpec(memory_space=pltpu.VMEM)
SMEM = pl.BlockSpec(memory_space=pltpu.SMEM)
ANY = pl.BlockSpec(memory_space=pl.ANY)


def dot(a, b):
    return jnp.dot(a, b, preferred_element_type=F32)


def dot_nt(a, b):
    return lax.dot_general(a, b, (((1,), (1,)), ((), ())), preferred_element_type=F32)


def dot_tn(a, b):
    return lax.dot_general(a, b, (((0,), (0,)), ((), ())), preferred_element_type=F32)


def target(me, block, experts):
    inner = experts // (2 * RING)
    place = (me // (2 * inner) + block // inner) % RING
    return (place * inner + (me // 2 % inner ^ block % inner)) * 2 + me % 2


def pack_kernel(me_ref, *refs):
    me = me_ref[0]
    sources, out_refs = (refs[0:3], refs[3:6]), refs[6:]
    top, toks = refs[0].shape
    width, hidden = refs[1].shape[1], refs[2].shape[1]
    half = (width + hidden) // 2
    base, split = width + hidden, width - half
    span = len(sources) * MAIN
    rows = len(out_refs) * span
    row = lax.broadcasted_iota(jnp.int32, (rows, toks), 0)
    ids = target(me, row // span, 2 * len(out_refs))
    sub = row % MAIN
    low = sub < MAIN // 2
    earlier = lax.broadcasted_iota(jnp.int32, (toks, toks), 0) < lax.broadcasted_iota(
        jnp.int32, (toks, toks), 1
    )
    earlier = jnp.where(earlier, 1.0, 0.0).astype(BF16)
    picks, lows, highs = [], [], []
    full, full_rest = 0.0, 0.0
    for n, (routes_ref, _, _) in enumerate(sources):
        mine = row // MAIN % len(sources) == n
        chosen = jnp.zeros((rows, toks), F32)
        for k in range(top):
            chosen += jnp.where((routes_ref[k : k + 1, :] == ids) & mine, 1.0, 0.0)
        slot = jnp.where(chosen > 0.0, dot(chosen.astype(BF16), earlier), -1.0).astype(jnp.int32)
        pick = jnp.where(slot == sub, 1.0, 0.0)
        rest = jnp.where(slot == jnp.where(low, MAIN + sub, MAIN // 2 + sub), 1.0, 0.0)
        full += jnp.sum(pick, axis=1, keepdims=True)
        full_rest += jnp.sum(rest, axis=1, keepdims=True)
        picks.append(pick.astype(BF16))
        lows.append(jnp.where(low, rest, 0.0).astype(BF16))
        highs.append(jnp.where(low, 0.0, rest).astype(BF16))
    lane0 = lax.broadcasted_iota(jnp.int32, (rows, 128), 1) == 0
    low_lanes = lax.broadcasted_iota(jnp.int32, (rows, 128), 0) % MAIN < MAIN // 2

    def put(at, value):
        for q, ref in enumerate(out_refs):
            ref[:, at : at + value.shape[1]] = value[q * span : (q + 1) * span].astype(BF16)

    def x(which, cols):
        return sum(dot(w, refs[cols]) for w, (_, refs, _) in zip(which, sources))

    def y(which):
        return sum(dot(w, ref[...]) for w, (_, _, ref) in zip(which, sources))

    first = x(picks, (slice(None), slice(0, 128)))
    put(0, jnp.where(lane0 & (full == 0.0), EMPTY, first))
    put(128, x(picks, (slice(None), slice(128, width))))
    put(width, y(picks))
    rem = x(lows, (slice(None), slice(0, split))) + x(highs, (slice(None), slice(half, width)))
    put(base, jnp.where(lane0 & low_lanes & (full_rest == 0.0), EMPTY, rem[:, :128]))
    put(base + 128, rem[:, 128:])
    put(base + split, x(lows, (slice(None), slice(split, half))) + y(highs))


def pack(me, mine, other, blocks):
    toks, width = mine[1].shape
    width = (width + mine[2].shape[1]) * CAP // MAIN
    return pl.pallas_call(
        pack_kernel,
        name="pack",
        out_shape=[jax.ShapeDtypeStruct((2 * MAIN, width), BF16)] * blocks,
        in_specs=[SMEM] + [VMEM] * 6,
        out_specs=[VMEM] * blocks,
        compiler_params=pltpu.CompilerParams(vmem_limit_bytes=12 * 2**20),
        cost_estimate=pl.CostEstimate(
            flops=8 * blocks * MAIN * toks * width, bytes_accessed=3 * 2**20, transcendentals=0
        ),
    )(me, *mine, *other)


def fold_kernel(rep_ref, p_ref, s_ref, *refs):
    out_ref = refs[-1]
    half = p_ref.shape[1]
    p, s = p_ref[0].astype(F32), s_ref[0].astype(F32)
    row = lax.broadcasted_iota(jnp.int32, (half, half), 0)
    col = lax.broadcasted_iota(jnp.int32, (half, half), 1)
    out_ref[:half, :] = jnp.where(col >= row, p, s).astype(BF16)
    diagonal = jnp.sum(jnp.where(row == col, s, 0.0), axis=0, keepdims=True)
    out_ref[half : half + PAD, :] = jnp.broadcast_to(diagonal, (PAD, half)).astype(BF16)
    if len(refs) > 1:
        out_ref[half + PAD :, :] = refs[0][0]


def fold(rep, a_inverse):
    half = a_inverse.shape[1] // 2
    rows = half + PAD + AHEAD
    extra = [pl.BlockSpec((1, AHEAD, half), lambda i, rep: (0, 0, 2 * rep[0] + 1))] if AHEAD else []
    return pl.pallas_call(
        fold_kernel,
        name="fold",
        out_shape=jax.ShapeDtypeStruct((rows, half), BF16),
        grid_spec=pltpu.PrefetchScalarGridSpec(
            num_scalar_prefetch=1,
            grid=(1,),
            in_specs=[
                pl.BlockSpec((1, half, half), lambda i, rep: (0, 0, 2 * rep[0])),
                pl.BlockSpec((1, half, half), lambda i, rep: (0, 1, 2 * rep[0] + 1)),
                *extra,
            ],
            out_specs=pl.BlockSpec((rows, half), lambda i, rep: (0, 0)),
        ),
        compiler_params=pltpu.CompilerParams(vmem_limit_bytes=12 * 2**20),
        cost_estimate=pl.CostEstimate(flops=half * half, bytes_accessed=6 * half * half, transcendentals=0),
    )(rep, *[a_inverse] * (2 + len(extra)))


def square_kernel(rep_ref, q_ref, out_ref):
    out_ref[...] = q_ref[0, AHEAD:, :]


def square_of(rep, a_inverse):
    half = a_inverse.shape[1] // 2
    return pl.pallas_call(
        square_kernel,
        name="square",
        out_shape=jax.ShapeDtypeStruct((half - AHEAD, half), BF16),
        grid_spec=pltpu.PrefetchScalarGridSpec(
            num_scalar_prefetch=1,
            grid=(1,),
            in_specs=[pl.BlockSpec((1, half, half), lambda i, rep: (0, 0, 2 * rep[0] + 1))],
            out_specs=pl.BlockSpec((half - AHEAD, half), lambda i, rep: (0, 0)),
        ),
        compiler_params=pltpu.CompilerParams(vmem_limit_bytes=6 * 2**20),
        cost_estimate=pl.CostEstimate(flops=half * half, bytes_accessed=2 * half * half, transcendentals=0),
    )(rep, a_inverse)


def gather_rows(groups, x_ref, y_ref, at):
    cols = x_ref.shape[2]
    width = 2 * cols
    hidden = y_ref.shape[1]
    half = (width + hidden) // 2
    base = width + hidden
    start = at
    for ref in groups:
        count = ref.shape[0]
        x_ref[0, at : at + count, :] = ref[:, :cols]
        x_ref[1, at : at + count, :] = ref[:, cols:width]
        y_ref[at : at + count, :] = ref[:, width:base]
        at += count
    for ref in groups:
        count = ref.shape[0] // 2
        low = lax.broadcasted_iota(jnp.int32, (count, half), 0) % MAIN < MAIN // 2
        one, two = ref[:count, base:].astype(F32), ref[count:, base:].astype(F32)
        lo = jnp.where(low, one, pltpu.roll(two, MAIN // 2, 0)).astype(BF16)
        hi = jnp.where(low, pltpu.roll(one, count - MAIN // 2, 0), two).astype(BF16)
        x_ref[0, at : at + count, :] = lo[:, :cols]
        x_ref[1, at : at + count, : half - cols] = lo[:, cols:]
        x_ref[1, at : at + count, half - cols :] = hi[:, : width - half]
        y_ref[at : at + count, :] = hi[:, width - half :]
        at += count
    edge = x_ref[0, start:at, :128].astype(F32)
    empty = (lax.broadcasted_iota(jnp.int32, edge.shape, 1) == 0) & (edge == EMPTY)
    x_ref[0, start:at, :128] = jnp.where(empty, 0.0, edge).astype(BF16)
    return (at - start) - jnp.sum(jnp.where(empty, 1.0, 0.0))


def mix_rows(x_ref, rows, a_ref, ps_ref, rep, own_ref, part_ref):
    oth = 1 - rep
    side = x_ref.shape[2]
    half = side // 2
    own_at, oth_at = pl.multiple_of(rep * side, side), pl.multiple_of(oth * side, side)
    x_own, x_oth = x_ref[rep, rows, :], x_ref[oth, rows, :]
    for c in range(side // TILE):
        cols = slice(c * TILE, (c + 1) * TILE)
        own_ref[rows, cols] = (
            dot(x_own, a_ref[0, :, pl.ds(own_at + c * TILE, TILE)])
            + dot_nt(x_oth, a_ref[0, cols, pl.ds(oth_at, side)])
        ).astype(BF16)
    for c in range(side // TILE):
        h, inner = divmod(c * TILE, half)
        value = dot(x_own, a_ref[0, :, pl.ds(oth_at + c * TILE, TILE)]) + dot(
            x_oth[:, h * half : (h + 1) * half], ps_ref[h, :, inner : inner + TILE]
        )
        if h == 1 and AHEAD:
            value += dot(x_oth[:, :AHEAD], ps_ref[2, :AHEAD, inner : inner + TILE])
        if c * TILE < AHEAD:
            value += dot_nt(x_oth[:, half:], ps_ref[2, inner : inner + TILE, :])
            own_ref[rows, side + c * TILE : side + (c + 1) * TILE] = value.astype(BF16)
        else:
            part_ref[rows, c * TILE - AHEAD : (c + 1) * TILE - AHEAD] = value


def early_kernel(rep_ref, *refs, groups, unfold):
    blocks = refs[:groups]
    tri_ref, g_ref, a_ref, x_ref, y_ref, own_ref, part_ref, v_ref, count_ref = refs[groups : groups + 9]
    ps_ref = refs[-1]
    rep = rep_ref[0]
    half = tri_ref.shape[1]
    if unfold:
        if AHEAD:
            ps_ref[2, :AHEAD, :] = tri_ref[half + PAD :, :]
        mix = tri_ref[:half, :].astype(F32)
        mix_t = mix.T
        row = lax.broadcasted_iota(jnp.int32, (half, half), 0)
        col = lax.broadcasted_iota(jnp.int32, (half, half), 1)
        diagonal = tri_ref[half : half + 1, :].astype(F32)
        ps_ref[0] = jnp.where(col >= row, mix, mix_t).astype(BF16)
        ps_ref[1] = jnp.where(col < row, mix, jnp.where(col == row, diagonal, mix_t)).astype(BF16)
    else:
        ps_ref = tri_ref
    count = gather_rows(blocks, x_ref, y_ref, 0)
    count_ref[...] = jnp.full(count_ref.shape, count, F32)
    v_ref[...] = dot(y_ref[...], g_ref[0]).astype(BF16)
    mix_rows(x_ref, slice(0, x_ref.shape[1]), a_ref, ps_ref, rep, own_ref, part_ref)


def early(rep, groups, tri, g_inverse, a_inverse, unfold):
    rows = sum(g.shape[0] for g in groups) * CAP // MAIN
    _, side, width = a_inverse.shape
    hidden = g_inverse.shape[1]
    half = side // 2
    tri_shape = [jax.ShapeDtypeStruct((3 if AHEAD else 2, half, half), BF16)] if unfold else []
    return pl.pallas_call(
        functools.partial(early_kernel, groups=len(groups), unfold=unfold),
        name="early",
        out_shape=[
            jax.ShapeDtypeStruct((2, rows, side), BF16),
            jax.ShapeDtypeStruct((rows, hidden), BF16),
            jax.ShapeDtypeStruct((rows, side + AHEAD), BF16),
            jax.ShapeDtypeStruct((rows, side - AHEAD), F32),
            jax.ShapeDtypeStruct((rows, hidden), BF16),
            jax.ShapeDtypeStruct((8, 128), F32),
        ]
        + tri_shape,
        in_specs=[SMEM] + [VMEM] * (len(groups) + 3),
        out_specs=[VMEM] * (6 + unfold),
        compiler_params=pltpu.CompilerParams(vmem_limit_bytes=20 * 2**20),
        cost_estimate=pl.CostEstimate(flops=4 * rows * width * side, bytes_accessed=2**23, transcendentals=0),
    )(rep, *groups, tri, g_inverse, a_inverse)


def main_kernel(rep_ref, owner_ref, *refs, bundles):
    done = [refs[6 * n : 6 * (n + 1)] for n in range(bundles)]
    (
        a_out, kept_out, u_out, part_ref, xo_ref, v_ref, inv_ref,
        x_ref, y_ref, own_ref, abuf, gbuf, ubuf, a_sem, g_sem, u_sem,
    ) = refs[6 * bundles :]
    rep = rep_ref[0]
    oth = 1 - rep
    side = x_ref.shape[2]
    at = 0
    count = 0.0
    for x_in, y_in, own_in, part_in, v_in, count_in in done:
        more = at + y_in.shape[0]
        x_ref[:, at:more, :] = x_in[...]
        y_ref[at:more, :] = y_in[...]
        own_ref[at:more, :] = own_in[...]
        part_ref[at:more, :] = part_in[...]
        v_ref[at:more, :] = v_in[...]
        count = count + count_in[...]
        at = more
    inv = 1.0 / count
    inv_ref[...] = inv
    inv = inv[:1, :1]

    writes = []
    for i in range(side // TILE):
        lhs = x_ref[rep, :, i * TILE : (i + 1) * TILE]
        for h in range(2):
            abuf[i, :, h * side : (h + 1) * side] = dot_tn(lhs, x_ref[h]) * inv
        write = pltpu.make_async_copy(abuf.at[i], a_out.at[0, pl.ds(i * TILE, TILE), :], a_sem.at[i])
        write.start()
        writes.append(write)

    keep = jnp.where(owner_ref[0] == rep, 1.0, 0.0) * inv
    gbuf[...] = dot_tn(y_ref[...], y_ref[...]) * keep
    write = pltpu.make_async_copy(gbuf, kept_out.at[0, 0], g_sem)
    write.start()
    writes.append(write)

    xo_ref[...] = x_ref[oth, :, AHEAD:]
    for c in range((side + AHEAD) // TILE):
        cols = slice(c * TILE, (c + 1) * TILE)
        ubuf[cols, :] = (dot_tn(own_ref[:, cols], v_ref[...]) * inv).astype(BF16)
        to = rep * side + c * TILE if c * TILE < side else oth * side + c * TILE - side
        write = pltpu.make_async_copy(
            ubuf.at[pl.ds(c * TILE, TILE)], u_out.at[0, pl.ds(to, TILE), :], u_sem.at[c]
        )
        write.start()
        writes.append(write)
    for write in writes:
        write.wait()


def products(rep, owner, done, a_shape, hidden):
    rows = sum(d[1].shape[0] for d in done)
    _, side, width = a_shape
    return pl.pallas_call(
        functools.partial(main_kernel, bundles=len(done)),
        name="products",
        out_shape=[
            jax.ShapeDtypeStruct((1, side, width), F32),
            jax.ShapeDtypeStruct((1, 1, hidden, hidden), F32),
            jax.ShapeDtypeStruct((1, width, hidden), BF16),
            jax.ShapeDtypeStruct((rows, side - AHEAD), F32),
            jax.ShapeDtypeStruct((rows, side - AHEAD), BF16),
            jax.ShapeDtypeStruct((rows, hidden), BF16),
            jax.ShapeDtypeStruct((8, 128), F32),
        ],
        in_specs=[SMEM, SMEM] + [VMEM] * (6 * len(done)),
        out_specs=[ANY, ANY, ANY, VMEM, VMEM, VMEM, VMEM],
        scratch_shapes=[
            pltpu.VMEM((2, rows, side), BF16),
            pltpu.VMEM((rows, hidden), BF16),
            pltpu.VMEM((rows, side + AHEAD), BF16),
            pltpu.VMEM((side // TILE, TILE, width), F32),
            pltpu.VMEM((hidden, hidden), F32),
            pltpu.VMEM((side + AHEAD, hidden), BF16),
            pltpu.SemaphoreType.DMA((side // TILE,)),
            pltpu.SemaphoreType.DMA,
            pltpu.SemaphoreType.DMA(((side + AHEAD) // TILE,)),
        ],
        compiler_params=pltpu.CompilerParams(vmem_limit_bytes=36 * 2**20),
        cost_estimate=pl.CostEstimate(
            flops=4 * rows * width * side, bytes_accessed=12 * 2**20, transcendentals=0
        ),
    )(rep, owner, *[value for d in done for value in d])


def last_kernel(rep_ref, square_ref, part_ref, x_ref, v_ref, inv_ref, u_in, u_out, ubuf, u_sem):
    oth = 1 - rep_ref[0]
    rest, half = square_ref.shape
    side = 2 * half
    inv = inv_ref[:1, :1]
    stores = []
    for c in range((half + rest) // TILE):
        cols = slice(c * TILE, (c + 1) * TILE)
        at = c * TILE - rest
        if at < 0:
            extra = dot_nt(x_ref[:, rest:], square_ref[cols, :])
        else:
            extra = dot(x_ref[:, :rest], square_ref[:, at : at + TILE])
        mixed = (part_ref[:, cols] + extra).astype(BF16)
        ubuf[cols, :] = (dot_tn(mixed, v_ref[...]) * inv).astype(BF16)
        store = pltpu.make_async_copy(
            ubuf.at[pl.ds(c * TILE, TILE)],
            u_out.at[0, pl.ds(oth * side + half - rest + c * TILE, TILE), :],
            u_sem.at[c],
        )
        store.start()
        stores.append(store)
    for store in stores:
        store.wait()


def finish(rep, square, part, x, v, inv, u):
    side, hidden = part.shape[1], v.shape[1]
    return pl.pallas_call(
        last_kernel,
        name="finish",
        out_shape=jax.ShapeDtypeStruct(u.shape, BF16),
        in_specs=[SMEM] + [VMEM] * 5 + [ANY],
        out_specs=ANY,
        input_output_aliases={6: 0},
        scratch_shapes=[
            pltpu.VMEM((side, hidden), BF16),
            pltpu.SemaphoreType.DMA((side // TILE,)),
        ],
        compiler_params=pltpu.CompilerParams(vmem_limit_bytes=16 * 2**20),
        cost_estimate=pl.CostEstimate(
            flops=2 * part.shape[0] * side * (side + hidden), bytes_accessed=4 * 2**20, transcendentals=0
        ),
    )(rep, square, part, x, v, inv, u)


def parts(experts):
    inner = experts // (2 * RING)
    half = inner // 2
    return [
        list(range(inner)),
        [s * inner + w for s in (1, 3) for w in range(half)],
        [s * inner + w for s in (1, 3) for w in range(half, inner)],
        list(range(2 * inner, 3 * inner)),
    ]


def local(tokens, cotangents, routes, owner, a_inverse, g_inverse):
    experts = lax.axis_size("expert")
    me = lax.axis_index("expert").astype(jnp.int32).reshape(1)
    rep = lax.axis_index("replica").astype(jnp.int32).reshape(1)

    def swap(value):
        return lax.ppermute(value, "replica", [(0, 1), (1, 0)])

    def trade(value, to):
        return lax.ppermute(value, "expert", [(i, to(i)) for i in range(experts)])

    tri = swap(fold(rep, a_inverse))
    mine = (routes.T, tokens, cotangents)
    other = tuple(trade(value, lambda i: i ^ 1) for value in mine)
    blocks = pack(me, mine, other, experts // 2)
    got = [blocks[0]]
    for q in range(1, experts // 2):
        got.append(trade(blocks[q], lambda i, q=q: target(i, q, experts)))
    groups = [jnp.concatenate([got[q] for q in part], axis=0) for part in parts(experts)]
    others = [swap(group) for group in groups]
    square = square_of(rep, a_inverse)
    square = swap(square)
    *first, ps = early(rep, groups, tri, g_inverse, a_inverse, True)
    second = early(rep, others[:3], ps, g_inverse, a_inverse, False)
    third = early(rep, others[3:], ps, g_inverse, a_inverse, False)
    a_factor, kept, u, part, xo, v, inv = products(
        rep, owner, (first, second, third), a_inverse.shape, g_inverse.shape[1]
    )
    return a_factor, kept, finish(rep, square, part, xo, v, inv, u)


def slot_table(route_block, expert_count, capacity):
    top_k = route_block.shape[1]
    route_ids = route_block.reshape(-1)
    in_window = route_ids < expert_count
    columns = lax.broadcasted_iota(jnp.int32, (route_ids.shape[0], expert_count), 1)
    one_hot = ((route_ids[:, None] == columns) & in_window[:, None]).astype(jnp.int32)
    before = jnp.cumsum(one_hot, axis=0) - one_hot
    position = jnp.sum(before * one_hot, axis=1)
    sentinel = expert_count * capacity
    slot_ids = jnp.where(in_window, route_ids * capacity + position, sentinel)
    source_ids = jnp.arange(route_ids.shape[0], dtype=jnp.int32) // top_k
    slot_token = jnp.zeros((sentinel + 1,), jnp.int32).at[slot_ids].set(source_ids)
    filled = jnp.zeros((sentinel + 1,), jnp.int32).at[slot_ids].set(1)
    return (slot_token[:sentinel], filled[:sentinel])


def local_any(tokens, cotangents, routes, owner, a_inverse, g_inverse):
    expert_count = lax.axis_size("expert")
    replica_count = lax.axis_size("replica")
    width = tokens.shape[1]
    hidden_width = cotangents.shape[1]
    slot_token, filled = slot_table(routes, expert_count, CAP)
    slot_mask = filled.astype(jnp.bfloat16)[:, None]
    send_x = (jnp.take(tokens, slot_token, axis=0) * slot_mask).reshape(expert_count, CAP, width)
    send_y = (jnp.take(cotangents, slot_token, axis=0) * slot_mask).reshape(
        expert_count, CAP, hidden_width
    )
    sent_counts = jnp.sum(filled.reshape(expert_count, CAP), axis=1).astype(jnp.bfloat16)
    recv_x, recv_y, recv_counts = (
        lax.all_to_all(send_x, "expert", split_axis=0, concat_axis=0, tiled=True),
        lax.all_to_all(send_y, "expert", split_axis=0, concat_axis=0, tiled=True),
        lax.all_to_all(sent_counts, "expert", split_axis=0, concat_axis=0, tiled=True),
    )
    rows_x = recv_x.reshape(-1, width)
    rows_y = recv_y.reshape(-1, hidden_width)
    block_rows = width // replica_count
    own_start = lax.axis_index("replica") * block_rows
    piece_x = lax.all_gather(rows_x, "replica", axis=0, tiled=True)
    piece_y = lax.all_gather(rows_y, "replica", axis=0, tiled=True)
    piece_counts = lax.all_gather(recv_counts, "replica", axis=0, tiled=True)
    columns = lax.dynamic_slice_in_dim(piece_x, own_start, block_rows, 1)
    a_next = jnp.dot(columns.T, piece_x, preferred_element_type=jnp.float32)
    g_next = jnp.dot(piece_y.T, piece_y, preferred_element_type=jnp.float32)
    count_next = jnp.sum(piece_counts.astype(jnp.float32))
    mixed_own = jnp.dot(a_inverse[0], piece_x.T, preferred_element_type=jnp.float32).astype(BF16)
    mixed = lax.all_gather(mixed_own, "replica", axis=0, tiled=True)
    right = jnp.dot(piece_y, g_inverse[0], preferred_element_type=jnp.float32).astype(BF16)
    update = (jnp.dot(mixed, right, preferred_element_type=jnp.float32) / count_next).astype(BF16)
    a_factor = (a_next / count_next)[None]
    keeper = owner[0] == lax.axis_index("replica")
    kept = jnp.where(keeper, g_next / count_next, jnp.zeros_like(g_next))[None, None]
    return (a_factor, kept, update[None])


def solution(mesh):
    placed = (
        P(("expert", "replica"), None),
        P(("expert", "replica"), None),
        P(("expert", "replica"), None),
        P("expert"),
        P("expert", "replica", None),
        P("expert", None, None),
    )
    pair = mesh.shape["replica"] == 2
    return jax.shard_map(
        local if pair else local_any,
        mesh=mesh,
        in_specs=placed,
        out_specs=(
            P("expert", "replica", None),
            P("replica", "expert", None, None),
            P("expert", None, None),
        ),
        check_vma=False,
    )
```

time: 209 us -> 69.8 us (0.33)
  the two profiles are of different devices: /device:TPU:0 before, /device:TPU:24 now
where the time goes in v1:
time: 69.8 us; the launch traced here: 69.5 us
  starting transfers between devices  27.6 us (40%)
  waiting for transfers between devices  19.7 us (28%)
  Pallas kernels  15.8 us (23%)
  local copies, waits for them, and re-layouts  4.94 us (7%)
  between operations  1.58 us (2%)
    ppermute x10, starting transfers between devices, trade(): return lax.ppermute(value, 'expert', [(i, to(i)) for i in range(experts)])  20.5 us
    ppermute x6, waiting for transfers between devices, swap(): return lax.ppermute(value, 'replica', [(0, 1), (1, 0)])  12.3 us
    ppermute x10, waiting for transfers between devices, trade(): return lax.ppermute(value, 'expert', [(i, to(i)) for i in range(experts)])  7.42 us
    ppermute x6, starting transfers between devices, swap(): return lax.ppermute(value, 'replica', [(0, 1), (1, 0)])  7.1 us
    pallas_call x3, Pallas kernels, early(): pl.pallas_call(functools.partial(early_kernel, groups=len(groups), unfold...  6.11 us
    pallas_call x1, Pallas kernels, products(): pl.pallas_call(functools.partial(main_kernel, bundles=len(done)), name='p...  6.03 us
    unnamed x18, local copies, waits for them, and re-layouts  4.88 us
    pallas_call x1, Pallas kernels, finish(): pl.pallas_call(last_kernel, name='finish', out_shape=jax.ShapeDtypeStruct...  2.41 us
  transfers between devices with their start and end apart: 16, of which 6 were waited for; matrix products, arithmetic and copies ran while one was open for 0% of the time, Pallas kernels for 19%

profile of v1, /device:TPU:24, one launch (start us, length us, event | category | flops | bytes accessed | tf_op | source)
XLA Modules:
  0.0 69.5 jit_solution(1237437523984802471)
XLA Ops:
  0.6 0.1 collective-permute-start.1
  0.7 0.5 collective-permute-start.2
  1.2 0.1 collective-permute-start
  1.3 0.0 copy-start
  1.3 2.2 %copy-done = bf16[1,1024,2048]{2,1,0:T(8,128)(2,1)S(1)} copy-done((bf16[1,1024,2048]{2,1,0:T(8,128)(2,1)S(1)}, bf16[1,1024,2048]{2,1,0:T(8,128)(2,1)}, u32[]{:S(2)}) %copy-start) | copy-done | bytes 4194328
  3.5 0.0 copy-start.4
  3.5 0.1 fold.1
  3.6 1.6 %collective-permute-start.10 = (bf16[784,512]{1,0:T(8,128)(2,1)S(1)}, bf16[784,512]{1,0:T(8,128)(2,1)S(1)}, u32[]{:S(2)}, u32[]{:S(2)}) collective-permute-start(bf16[784,512]{1,0:T(8,128)(2,1)S(1)} %fold.1), channel_id=1, source_target_pairs={{0,1},{1,0},{2,3},{3,2},{4,5},{5,4},{6,7},{7,6},{8,9},{9,8},{10,11... | collective-permute-start | bytes 2408456 | tf_op jit(solution)/shard_map/ppermute | solution.py:430
  5.1 0.0 collective-permute-done.refs_3_
  5.1 0.0 collective-permute-done.2.refs_5_
  5.1 0.0 collective-permute-done.1.refs_4_
  5.2 0.0 copy-done.4
  5.2 0.0 copy-done.5
  5.2 0.0 copy-done.6
  5.2 1.1 %pack.1 = (bf16[16,4224]{1,0:T(8,128)(2,1)S(1)}, bf16[16,4224]{1,0:T(8,128)(2,1)S(1)}, bf16[16,4224]{1,0:T(8,128)(2,1)S(1)}, bf16[16,4224]{1,0:T(8,128)(2,1)S(1)...) custom-call(s32[1]{0:T(128)} %bitcast.1.me_ref, ...), custom_call_target="tpu_custom_call" | custom-call | flops 276824064 | bytes 3145728 | tf_op jit(solution)/shard_map/pack/pallas_call | solution.py:104
  6.3 0.4 collective-permute-start.8
  6.7 3.5 %collective-permute-start.9 = (bf16[16,4224]{1,0:T(8,128)(2,1)S(1)}, bf16[16,4224]{1,0:T(8,128)(2,1)S(1)}, u32[]{:S(2)}, u32[]{:S(2)}) collective-permute-start(bf16[16,4224]{1,0:T(8,128)(2,1)S(1)} %get-tuple-element.44), channel_id=1, source_target_pairs={{0,20},{2,22},{4,16},{6,18},{8,28},{10,30},{12,24},{14,26},{16,4},... | collective-permute-start | bytes 405512 | tf_op jit(solution)/shard_map/ppermute | solution.py:433
  10.2 0.2 collective-permute-start.6
  10.4 2.8 %collective-permute-start.7 = (bf16[16,4224]{1,0:T(8,128)(2,1)S(1)}, bf16[16,4224]{1,0:T(8,128)(2,1)S(1)}, u32[]{:S(2)}, u32[]{:S(2)}) collective-permute-start(bf16[16,4224]{1,0:T(8,128)(2,1)S(1)} %get-tuple-element.42), channel_id=1, source_target_pairs={{0,28},{2,30},{4,24},{6,26},{8,4},{10,6},{12,0},{14,2},{16,12},{18... | collective-permute-start | bytes 405512 | tf_op jit(solution)/shard_map/ppermute | solution.py:433
  13.2 6.2 %collective-permute-done.8 = bf16[16,4224]{1,0:T(8,128)(2,1)S(1)} collective-permute-done((bf16[16,4224]{1,0:T(8,128)(2,1)S(1)}, bf16[16,4224]{1,0:T(8,128)(2,1)S(1)}, u32[]{:S(2)}, u32[]{:S(2)}) %collective-permute-start.8) | collective-permute-done | bytes 135200 | tf_op jit(solution)/shard_map/ppermute | solution.py:433
  19.4 3.3 %collective-permute-start.4 = (bf16[16,4224]{1,0:T(8,128)(2,1)S(1)}, bf16[16,4224]{1,0:T(8,128)(2,1)S(1)}, u32[]{:S(2)}, u32[]{:S(2)}) collective-permute-start(bf16[16,4224]{1,0:T(8,128)(2,1)S(1)} %get-tuple-element.39), channel_id=1, source_target_pairs={{0,8},{2,10},{4,12},{6,14},{8,16},{10,18},{12,20},{14,22},{16,24},... | collective-permute-start | bytes 405512 | tf_op jit(solution)/shard_map/ppermute | solution.py:433
  22.7 0.0 collective-permute-done.6
  22.7 9.0 %collective-permute-start.5 = (bf16[16,4224]{1,0:T(8,128)(2,1)S(1)}, bf16[16,4224]{1,0:T(8,128)(2,1)S(1)}, u32[]{:S(2)}, u32[]{:S(2)}) collective-permute-start(bf16[16,4224]{1,0:T(8,128)(2,1)S(1)} %get-tuple-element.40), channel_id=1, source_target_pairs={{0,24},{2,26},{4,28},{6,30},{8,0},{10,2},{12,4},{14,6},{16,8},{18,... | collective-permute-start | bytes 405512 | tf_op jit(solution)/shard_map/ppermute | solution.py:433
  31.8 0.0 collective-permute-done.9
  31.8 0.6 collective-permute-start.3
  32.4 0.0 collective-permute-done.7
  32.4 1.2 %collective-permute-start.14 = (bf16[32,4224]{1,0:T(8,128)(2,1)S(1)}, bf16[32,4224]{1,0:T(8,128)(2,1)S(1)}, u32[]{:S(2)}, u32[]{:S(2)}) collective-permute-start(bf16[32,4224]{1,0:T(8,128)(2,1)S(1)} %constant_dynamic-update-slice_fusion.6.refs_3_), channel_id=1, source_target_pairs={{0,1},{1,0},{2,3},{3,2},{4,5},{5,4},{6,7},{7,6},{8,9},{9,8},{10,11... | collective-permute-start | bytes 811016 | tf_op jit(solution)/shard_map/ppermute | solution.py:430
  33.6 0.0 collective-permute-done.4
  33.6 1.0 %collective-permute-start.13 = (bf16[32,4224]{1,0:T(8,128)(2,1)S(1)}, bf16[32,4224]{1,0:T(8,128)(2,1)S(1)}, u32[]{:S(2)}, u32[]{:S(2)}) collective-permute-start(bf16[32,4224]{1,0:T(8,128)(2,1)S(1)} %constant_dynamic-update-slice_fusion.4.refs_2_), channel_id=1, source_target_pairs={{0,1},{1,0},{2,3},{3,2},{4,5},{5,4},{6,7},{7,6},{8,9},{9,8},{10,11... | collective-permute-start | bytes 811016 | tf_op jit(solution)/shard_map/ppermute | solution.py:430
  34.6 0.2 collective-permute-done.5
  34.8 1.2 %collective-permute-start.12 = (bf16[32,4224]{1,0:T(8,128)(2,1)S(1)}, bf16[32,4224]{1,0:T(8,128)(2,1)S(1)}, u32[]{:S(2)}, u32[]{:S(2)}) collective-permute-start(bf16[32,4224]{1,0:T(8,128)(2,1)S(1)} %constant_dynamic-update-slice_fusion.2.refs_1_), channel_id=1, source_target_pairs={{0,1},{1,0},{2,3},{3,2},{4,5},{5,4},{6,7},{7,6},{8,9},{9,8},{10,11... | collective-permute-start | bytes 811016 | tf_op jit(solution)/shard_map/ppermute | solution.py:430
  36.0 1.0 %collective-permute-done.3 = bf16[16,4224]{1,0:T(8,128)(2,1)S(1)} collective-permute-done((bf16[16,4224]{1,0:T(8,128)(2,1)S(1)}, bf16[16,4224]{1,0:T(8,128)(2,1)S(1)}, u32[]{:S(2)}, u32[]{:S(2)}) %collective-permute-start.3) | collective-permute-done | bytes 135200 | tf_op jit(solution)/shard_map/ppermute | solution.py:433
  37.1 1.2 %collective-permute-start.11 = (bf16[32,4224]{1,0:T(8,128)(2,1)S(1)}, bf16[32,4224]{1,0:T(8,128)(2,1)S(1)}, u32[]{:S(2)}, u32[]{:S(2)}) collective-permute-start(bf16[32,4224]{1,0:T(8,128)(2,1)S(1)} %constant_dynamic-update-slice_fusion.refs_0_), channel_id=1, source_target_pairs={{0,1},{1,0},{2,3},{3,2},{4,5},{5,4},{6,7},{7,6},{8,9},{9,8},{10,11... | collective-permute-start | bytes 811016 | tf_op jit(solution)/shard_map/ppermute | solution.py:430
  38.3 2.2 %copy-done.1 = bf16[1,1024,2048]{2,1,0:T(8,128)(2,1)S(1)} copy-done((bf16[1,1024,2048]{2,1,0:T(8,128)(2,1)S(1)}, bf16[1,1024,2048]{2,1,0:T(8,128)(2,1)}, u32[]{:S(2)}) %copy-start.1) | copy-done | bytes 4194328
  41.3 0.0 collective-permute-done.10.refs_4_
  41.3 0.9 %collective-permute-start.15 = (bf16[256,512]{1,0:T(8,128)(2,1)S(1)}, bf16[256,512]{1,0:T(8,128)(2,1)S(1)}, u32[]{:S(2)}, u32[]{:S(2)}) collective-permute-start(bf16[256,512]{1,0:T(8,128)(2,1)S(1)} %square.1), channel_id=1, source_target_pairs={{0,1},{1,0},{2,3},{3,2},{4,5},{5,4},{6,7},{7,6},{8,9},{9,8},{10,11... | collective-permute-start | bytes 786440 | tf_op jit(solution)/shard_map/ppermute | solution.py:430
  42.3 0.0 copy-done.3
  42.3 0.5 copy-done.2
  42.7 2.3 %early.3 = (bf16[2,192,1024]{2,1,0:T(8,128)(2,1)S(1)}, bf16[192,768]{1,0:T(8,128)(2,1)S(1)}, bf16[192,1280]{1,0:T(8,128)(2,1)S(1)}, f32[192,768]{1,0:T(8,128)S(1...) custom-call(s32[1]{0:T(128)} %bitcast.rep_ref, ...), custom_call_target="tpu_custom_call" | custom-call | flops 1610612736 | bytes 8388608 | tf_op jit(solution)/shard_map/early/pallas_call | solution.py:260
  45.0 0.0 collective-permute-done.14.refs_0_
  45.1 1.9 %early.5 = (bf16[2,48,1024]{2,1,0:T(8,128)(2,1)S(1)}, bf16[48,768]{1,0:T(8,128)(2,1)S(1)}, bf16[48,1280]{1,0:T(8,128)(2,1)S(1)}, f32[48,768]{1,0:T(8,128)S(1)}, ...) custom-call(s32[1]{0:T(128)} %bitcast.rep_ref, bf16[32,4224]{1,0:T(8,128)(2,1)S(1)} %collective-permute-done.14.refs_0_, ...), custom_call_target="tpu_custom_call" | custom-call | flops 402653184 | bytes 8388608 | tf_op jit(solution)/shard_map/early/pallas_call | solution.py:260
  47.0 0.7 collective-permute-done.13.refs_2_
  47.6 5.8 %collective-permute-done.12.refs_1_ = bf16[32,4224]{1,0:T(8,128)(2,1)S(1)} collective-permute-done((bf16[32,4224]{1,0:T(8,128)(2,1)S(1)}, bf16[32,4224]{1,0:T(8,128)(2,1)S(1)}, u32[]{:S(2)}, u32[]{:S(2)}) %collective-permute-start.12) | collective-permute-done | bytes 270368 | tf_op jit(solution)/shard_map/ppermute | solution.py:430
  53.4 5.8 %collective-permute-done.11.refs_0_ = bf16[32,4224]{1,0:T(8,128)(2,1)S(1)} collective-permute-done((bf16[32,4224]{1,0:T(8,128)(2,1)S(1)}, bf16[32,4224]{1,0:T(8,128)(2,1)S(1)}, u32[]{:S(2)}, u32[]{:S(2)}) %collective-permute-start.11) | collective-permute-done | bytes 270368 | tf_op jit(solution)/shard_map/ppermute | solution.py:430
  59.2 1.9 %early.4 = (bf16[2,144,1024]{2,1,0:T(8,128)(2,1)S(1)}, bf16[144,768]{1,0:T(8,128)(2,1)S(1)}, bf16[144,1280]{1,0:T(8,128)(2,1)S(1)}, f32[144,768]{1,0:T(8,128)S(1...) custom-call(s32[1]{0:T(128)} %bitcast.rep_ref, bf16[32,4224]{1,0:T(8,128)(2,1)S(1)} %collective-permute-done.11.refs_0_, ...), custom_call_target="tpu_custom_call" | custom-call | flops 1207959552 | bytes 8388608 | tf_op jit(solution)/shard_map/early/pallas_call | solution.py:260
  61.1 6.0 %products.1 = (f32[1,1024,2048]{2,1,0:T(8,128)}, f32[1,1,768,768]{3,2,1,0:T(8,128)}, bf16[1,2048,768]{2,1,0:T(8,128)(2,1)}, f32[384,768]{1,0:T(8,128)S(1)}, bf16...) custom-call(s32[1]{0:T(128)} %bitcast.rep_ref, s32[1]{0:T(128)S(6)} %copy.15.owner_ref, ...), custom_call_target="tpu_custom_call" | custom-call | flops 3221225472 | bytes 12582912 | tf_op jit(solution)/shard_map/products/pallas_call | solution.py:335
  67.1 0.0 collective-permute-done.15.square_ref
  67.1 2.4 %finish.1 = bf16[1,2048,768]{2,1,0:T(8,128)(2,1)} custom-call(s32[1]{0:T(128)} %bitcast.rep_ref, bf16[256,512]{1,0:T(8,128)(2,1)S(1)} %collective-permute-done.15.square_ref, f32[384,768]{1,0:T(8,128)S(1)} %get-tuple-element.66.part_ref, bf16[384,768]{1,0:T(8,128)(2,1)S(1)} %get-tuple-element.67.x_ref, ...), custom_call_target="tpu_custom_call", output_to_operand_aliasing={{}: (6, {})} | custom-call | flops 905969664 | bytes 4194304 | tf_op jit(solution)/shard_map/finish/pallas_call | solution.py:395
  (14 shorter events, 0.1 us)
Async XLA Ops:
  0.6 4.5 %collective-permute-start.1 = (bf16[128,2048]{1,0:T(8,128)(2,1)}, bf16[128,2048]{1,0:T(8,128)(2,1)S(1)}, u32[]{:S(2)}, u32[]{:S(2)}) collective-permute-start(bf16[128,2048]{1,0:T(8,128)(2,1)} %refs_1_.1), channel_id=1, source_target_pairs={{0,2},{2,0},{4,6},{6,4},{8,10},{10,8},{12,14},{14,12},{16,18},{18,... | collective-permute-start | bytes 1572872 | tf_op jit(solution)/shard_map/ppermute | solution.py:433
  0.7 4.4 %collective-permute-start.2 = (bf16[128,768]{1,0:T(8,128)(2,1)}, bf16[128,768]{1,0:T(8,128)(2,1)S(1)}, u32[]{:S(2)}, u32[]{:S(2)}) collective-permute-start(bf16[128,768]{1,0:T(8,128)(2,1)} %refs_2_.2), channel_id=1, source_target_pairs={{0,2},{2,0},{4,6},{6,4},{8,10},{10,8},{12,14},{14,12},{16,18},{18,... | collective-permute-start | bytes 589832 | tf_op jit(solution)/shard_map/ppermute | solution.py:433
  1.2 3.9 %collective-permute-start = (s32[8,128]{1,0:T(8,128)}, s32[8,128]{1,0:T(8,128)S(1)}, u32[]{:S(2)}, u32[]{:S(2)}) collective-permute-start(s32[8,128]{1,0:T(8,128)} %bitcast.3), channel_id=1, source_target_pairs={{0,2},{2,0},{4,6},{6,4},{8,10},{10,8},{12,14},{14,12},{16,18},{18,... | collective-permute-start | bytes 12296 | tf_op jit(solution)/shard_map/ppermute | solution.py:433
  1.3 2.2 %copy-start = (bf16[1,1024,2048]{2,1,0:T(8,128)(2,1)S(1)}, bf16[1,1024,2048]{2,1,0:T(8,128)(2,1)}, u32[]{:S(2)}) copy-start(bf16[1,1024,2048]{2,1,0:T(8,128)(2,1)} %q_ref.1) | copy-start | bytes 12582916
  3.5 1.7 %copy-start.4 = (bf16[128,2048]{1,0:T(8,128)(2,1)S(1)}, bf16[128,2048]{1,0:T(8,128)(2,1)}, u32[]{:S(2)}) copy-start(bf16[128,2048]{1,0:T(8,128)(2,1)} %refs_1_.1) | copy-start | bytes 1572868
  3.5 1.7 %copy-start.5 = (bf16[128,768]{1,0:T(8,128)(2,1)S(1)}, bf16[128,768]{1,0:T(8,128)(2,1)}, u32[]{:S(2)}) copy-start(bf16[128,768]{1,0:T(8,128)(2,1)} %refs_2_.2) | copy-start | bytes 589828
  3.5 1.7 %copy-start.6 = (s32[128,8]{0,1:T(8,128)S(1)}, s32[128,8]{0,1:T(8,128)}, u32[]{:S(2)}) copy-start(s32[128,8]{0,1:T(8,128)} %param.8) | copy-start | bytes 12292
  3.6 37.7 %collective-permute-start.10 = (bf16[784,512]{1,0:T(8,128)(2,1)S(1)}, bf16[784,512]{1,0:T(8,128)(2,1)S(1)}, u32[]{:S(2)}, u32[]{:S(2)}) collective-permute-start(bf16[784,512]{1,0:T(8,128)(2,1)S(1)} %fold.1), channel_id=1, source_target_pairs={{0,1},{1,0},{2,3},{3,2},{4,5},{5,4},{6,7},{7,6},{8,9},{9,8},{10,11... | collective-permute-start | bytes 2408456 | tf_op jit(solution)/shard_map/ppermute | solution.py:430
  6.3 13.1 %collective-permute-start.8 = (bf16[16,4224]{1,0:T(8,128)(2,1)S(1)}, bf16[16,4224]{1,0:T(8,128)(2,1)S(1)}, u32[]{:S(2)}, u32[]{:S(2)}) collective-permute-start(bf16[16,4224]{1,0:T(8,128)(2,1)S(1)} %get-tuple-element.43), channel_id=1, source_target_pairs={{0,16},{2,18},{4,20},{6,22},{8,24},{10,26},{12,28},{14,30},{16,0},... | collective-permute-start | bytes 405512 | tf_op jit(solution)/shard_map/ppermute | solution.py:433
  6.7 25.1 %collective-permute-start.9 = (bf16[16,4224]{1,0:T(8,128)(2,1)S(1)}, bf16[16,4224]{1,0:T(8,128)(2,1)S(1)}, u32[]{:S(2)}, u32[]{:S(2)}) collective-permute-start(bf16[16,4224]{1,0:T(8,128)(2,1)S(1)} %get-tuple-element.44), channel_id=1, source_target_pairs={{0,20},{2,22},{4,16},{6,18},{8,28},{10,30},{12,24},{14,26},{16,4},... | collective-permute-start | bytes 405512 | tf_op jit(solution)/shard_map/ppermute | solution.py:433
  10.2 12.5 %collective-permute-start.6 = (bf16[16,4224]{1,0:T(8,128)(2,1)S(1)}, bf16[16,4224]{1,0:T(8,128)(2,1)S(1)}, u32[]{:S(2)}, u32[]{:S(2)}) collective-permute-start(bf16[16,4224]{1,0:T(8,128)(2,1)S(1)} %get-tuple-element.41), channel_id=1, source_target_pairs={{0,12},{2,14},{4,8},{6,10},{8,20},{10,22},{12,16},{14,18},{16,28},... | collective-permute-start | bytes 405512 | tf_op jit(solution)/shard_map/ppermute | solution.py:433
  10.4 22.0 %collective-permute-start.7 = (bf16[16,4224]{1,0:T(8,128)(2,1)S(1)}, bf16[16,4224]{1,0:T(8,128)(2,1)S(1)}, u32[]{:S(2)}, u32[]{:S(2)}) collective-permute-start(bf16[16,4224]{1,0:T(8,128)(2,1)S(1)} %get-tuple-element.42), channel_id=1, source_target_pairs={{0,28},{2,30},{4,24},{6,26},{8,4},{10,6},{12,0},{14,2},{16,12},{18... | collective-permute-start | bytes 405512 | tf_op jit(solution)/shard_map/ppermute | solution.py:433
  19.4 22.9 %copy-start.3 = (bf16[1,768,768]{2,1,0:T(8,128)(2,1)S(1)}, bf16[1,768,768]{2,1,0:T(8,128)(2,1)}, u32[]{:S(2)}) copy-start(bf16[1,768,768]{2,1,0:T(8,128)(2,1)} %refs_2_.3) | copy-start | bytes 3538948
  19.4 14.2 %collective-permute-start.4 = (bf16[16,4224]{1,0:T(8,128)(2,1)S(1)}, bf16[16,4224]{1,0:T(8,128)(2,1)S(1)}, u32[]{:S(2)}, u32[]{:S(2)}) collective-permute-start(bf16[16,4224]{1,0:T(8,128)(2,1)S(1)} %get-tuple-element.39), channel_id=1, source_target_pairs={{0,8},{2,10},{4,12},{6,14},{8,16},{10,18},{12,20},{14,22},{16,24},... | collective-permute-start | bytes 405512 | tf_op jit(solution)/shard_map/ppermute | solution.py:433
  22.7 12.0 %collective-permute-start.5 = (bf16[16,4224]{1,0:T(8,128)(2,1)S(1)}, bf16[16,4224]{1,0:T(8,128)(2,1)S(1)}, u32[]{:S(2)}, u32[]{:S(2)}) collective-permute-start(bf16[16,4224]{1,0:T(8,128)(2,1)S(1)} %get-tuple-element.40), channel_id=1, source_target_pairs={{0,24},{2,26},{4,28},{6,30},{8,0},{10,2},{12,4},{14,6},{16,8},{18,... | collective-permute-start | bytes 405512 | tf_op jit(solution)/shard_map/ppermute | solution.py:433
  31.8 5.2 %collective-permute-start.3 = (bf16[16,4224]{1,0:T(8,128)(2,1)S(1)}, bf16[16,4224]{1,0:T(8,128)(2,1)S(1)}, u32[]{:S(2)}, u32[]{:S(2)}) collective-permute-start(bf16[16,4224]{1,0:T(8,128)(2,1)S(1)} %get-tuple-element.38), channel_id=1, source_target_pairs={{0,4},{2,6},{4,0},{6,2},{8,12},{10,14},{12,8},{14,10},{16,20},{18,... | collective-permute-start | bytes 405512 | tf_op jit(solution)/shard_map/ppermute | solution.py:433
  32.4 12.6 %collective-permute-start.14 = (bf16[32,4224]{1,0:T(8,128)(2,1)S(1)}, bf16[32,4224]{1,0:T(8,128)(2,1)S(1)}, u32[]{:S(2)}, u32[]{:S(2)}) collective-permute-start(bf16[32,4224]{1,0:T(8,128)(2,1)S(1)} %constant_dynamic-update-slice_fusion.6.refs_3_), channel_id=1, source_target_pairs={{0,1},{1,0},{2,3},{3,2},{4,5},{5,4},{6,7},{7,6},{8,9},{9,8},{10,11... | collective-permute-start | bytes 811016 | tf_op jit(solution)/shard_map/ppermute | solution.py:430
  33.6 14.0 %collective-permute-start.13 = (bf16[32,4224]{1,0:T(8,128)(2,1)S(1)}, bf16[32,4224]{1,0:T(8,128)(2,1)S(1)}, u32[]{:S(2)}, u32[]{:S(2)}) collective-permute-start(bf16[32,4224]{1,0:T(8,128)(2,1)S(1)} %constant_dynamic-update-slice_fusion.4.refs_2_), channel_id=1, source_target_pairs={{0,1},{1,0},{2,3},{3,2},{4,5},{5,4},{6,7},{7,6},{8,9},{9,8},{10,11... | collective-permute-start | bytes 811016 | tf_op jit(solution)/shard_map/ppermute | solution.py:430
  34.8 18.6 %collective-permute-start.12 = (bf16[32,4224]{1,0:T(8,128)(2,1)S(1)}, bf16[32,4224]{1,0:T(8,128)(2,1)S(1)}, u32[]{:S(2)}, u32[]{:S(2)}) collective-permute-start(bf16[32,4224]{1,0:T(8,128)(2,1)S(1)} %constant_dynamic-update-slice_fusion.2.refs_1_), channel_id=1, source_target_pairs={{0,1},{1,0},{2,3},{3,2},{4,5},{5,4},{6,7},{7,6},{8,9},{9,8},{10,11... | collective-permute-start | bytes 811016 | tf_op jit(solution)/shard_map/ppermute | solution.py:430
  37.1 22.1 %collective-permute-start.11 = (bf16[32,4224]{1,0:T(8,128)(2,1)S(1)}, bf16[32,4224]{1,0:T(8,128)(2,1)S(1)}, u32[]{:S(2)}, u32[]{:S(2)}) collective-permute-start(bf16[32,4224]{1,0:T(8,128)(2,1)S(1)} %constant_dynamic-update-slice_fusion.refs_0_), channel_id=1, source_target_pairs={{0,1},{1,0},{2,3},{3,2},{4,5},{5,4},{6,7},{7,6},{8,9},{9,8},{10,11... | collective-permute-start | bytes 811016 | tf_op jit(solution)/shard_map/ppermute | solution.py:430
  38.3 2.2 %copy-start.1 = (bf16[1,1024,2048]{2,1,0:T(8,128)(2,1)S(1)}, bf16[1,1024,2048]{2,1,0:T(8,128)(2,1)}, u32[]{:S(2)}) copy-start(bf16[1,1024,2048]{2,1,0:T(8,128)(2,1)} %q_ref.1) | copy-start | bytes 12582916
  40.5 2.2 %copy-start.2 = (bf16[1,1024,2048]{2,1,0:T(8,128)(2,1)S(1)}, bf16[1,1024,2048]{2,1,0:T(8,128)(2,1)}, u32[]{:S(2)}) copy-start(bf16[1,1024,2048]{2,1,0:T(8,128)(2,1)} %q_ref.1) | copy-start | bytes 12582916
  41.3 25.8 %collective-permute-start.15 = (bf16[256,512]{1,0:T(8,128)(2,1)S(1)}, bf16[256,512]{1,0:T(8,128)(2,1)S(1)}, u32[]{:S(2)}, u32[]{:S(2)}) collective-permute-start(bf16[256,512]{1,0:T(8,128)(2,1)S(1)} %square.1), channel_id=1, source_target_pairs={{0,1},{1,0},{2,3},{3,2},{4,5},{5,4},{6,7},{7,6},{8,9},{9,8},{10,11... | collective-permute-start | bytes 786440 | tf_op jit(solution)/shard_map/ppermute | solution.py:430

commit v2 on v1

--- a/solution.py
+++ b/solution.py
@@ -12,10 +12,11 @@
 MAIN = 8
 EMPTY = 1024.0
 
-PAD = 16
+PAD = 8
 TILE = 256
 RING = 4
-AHEAD = 256
+FOLD_VMEM = 50 * 2**20
+AHEAD = 128
 
 
 F32 = jnp.float32
@@ -23,6 +24,10 @@
 VMEM = pl.BlockSpec(memory_space=pltpu.VMEM)
 SMEM = pl.BlockSpec(memory_space=pltpu.SMEM)
 ANY = pl.BlockSpec(memory_space=pl.ANY)
+
+
+def tiles(start, stop):
+    return [(at, min(at + TILE, stop)) for at in range(start, stop, TILE)]
 
 
 def dot(a, b):
@@ -114,40 +119,47 @@
     )(me, *mine, *other)
 
 
-def fold_kernel(rep_ref, p_ref, s_ref, *refs):
-    out_ref = refs[-1]
-    half = p_ref.shape[1]
-    p, s = p_ref[0].astype(F32), s_ref[0].astype(F32)
+def fold_kernel(rep_ref, a_hbm, out_ref, p_ref, s_ref, sems):
+    half = p_ref.shape[0]
+    at = pl.multiple_of(rep_ref[0] * 2 * half, 2 * half)
+    step = half // 4
+    loads = []
+    for top in range(0, half, step):
+        for ref, down, over in ((p_ref, 0, 0), (s_ref, half, half)):
+            src = a_hbm.at[0, pl.ds(down + top, step), pl.ds(at + over, half)]
+            loads.append(pltpu.make_async_copy(src, ref.at[pl.ds(top, step)], sems.at[len(loads)]))
+    if AHEAD:
+        src = a_hbm.at[0, pl.ds(0, AHEAD), pl.ds(at + half, half)]
+        loads.append(pltpu.make_async_copy(src, out_ref.at[pl.ds(half + PAD, AHEAD)], sems.at[len(loads)]))
+    for load in loads:
+        load.start()
     row = lax.broadcasted_iota(jnp.int32, (half, half), 0)
     col = lax.broadcasted_iota(jnp.int32, (half, half), 1)
+    for load in loads:
+        load.wait()
+    p, s = p_ref[...].astype(F32), s_ref[...].astype(F32)
     out_ref[:half, :] = jnp.where(col >= row, p, s).astype(BF16)
     diagonal = jnp.sum(jnp.where(row == col, s, 0.0), axis=0, keepdims=True)
     out_ref[half : half + PAD, :] = jnp.broadcast_to(diagonal, (PAD, half)).astype(BF16)
-    if len(refs) > 1:
-        out_ref[half + PAD :, :] = refs[0][0]
 
 
 def fold(rep, a_inverse):
     half = a_inverse.shape[1] // 2
     rows = half + PAD + AHEAD
-    extra = [pl.BlockSpec((1, AHEAD, half), lambda i, rep: (0, 0, 2 * rep[0] + 1))] if AHEAD else []
     return pl.pallas_call(
         fold_kernel,
         name="fold",
         out_shape=jax.ShapeDtypeStruct((rows, half), BF16),
-        grid_spec=pltpu.PrefetchScalarGridSpec(
-            num_scalar_prefetch=1,
-            grid=(1,),
-            in_specs=[
-                pl.BlockSpec((1, half, half), lambda i, rep: (0, 0, 2 * rep[0])),
-                pl.BlockSpec((1, half, half), lambda i, rep: (0, 1, 2 * rep[0] + 1)),
-                *extra,
-            ],
-            out_specs=pl.BlockSpec((rows, half), lambda i, rep: (0, 0)),
-        ),
-        compiler_params=pltpu.CompilerParams(vmem_limit_bytes=12 * 2**20),
+        in_specs=[SMEM, ANY],
+        out_specs=VMEM,
+        scratch_shapes=[
+            pltpu.VMEM((half, half), BF16),
+            pltpu.VMEM((half, half), BF16),
+            pltpu.SemaphoreType.DMA((9,)),
+        ],
+        compiler_params=pltpu.CompilerParams(vmem_limit_bytes=FOLD_VMEM),
         cost_estimate=pl.CostEstimate(flops=half * half, bytes_accessed=6 * half * half, transcendentals=0),
-    )(rep, *[a_inverse] * (2 + len(extra)))
+    )(rep, a_inverse)
 
 
 def square_kernel(rep_ref, q_ref, out_ref):
@@ -220,11 +232,12 @@
         )
         if h == 1 and AHEAD:
             value += dot(x_oth[:, :AHEAD], ps_ref[2, :AHEAD, inner : inner + TILE])
-        if c * TILE < AHEAD:
-            value += dot_nt(x_oth[:, half:], ps_ref[2, inner : inner + TILE, :])
-            own_ref[rows, side + c * TILE : side + (c + 1) * TILE] = value.astype(BF16)
-        else:
-            part_ref[rows, c * TILE - AHEAD : (c + 1) * TILE - AHEAD] = value
+        ready = min(max(AHEAD - c * TILE, 0), TILE)
+        if ready:
+            full = value[:, :ready] + dot_nt(x_oth[:, half:], ps_ref[2, inner : inner + ready, :])
+            own_ref[rows, side + c * TILE : side + c * TILE + ready] = full.astype(BF16)
+        if ready < TILE:
+            part_ref[rows, c * TILE + ready - AHEAD : (c + 1) * TILE - AHEAD] = value[:, ready:]
 
 
 def early_kernel(rep_ref, *refs, groups, unfold):
@@ -276,12 +289,14 @@
     )(rep, *groups, tri, g_inverse, a_inverse)
 
 
-def main_kernel(rep_ref, owner_ref, *refs, bundles):
-    done = [refs[6 * n : 6 * (n + 1)] for n in range(bundles)]
+def main_kernel(rep_ref, owner_ref, *refs, groups, bundles):
+    blocks = refs[:groups]
+    done = [refs[groups + 6 * n : groups + 6 * (n + 1)] for n in range(bundles)]
     (
+        ps_ref, g_ref, a_ref,
         a_out, kept_out, u_out, part_ref, xo_ref, v_ref, inv_ref,
         x_ref, y_ref, own_ref, abuf, gbuf, ubuf, a_sem, g_sem, u_sem,
-    ) = refs[6 * bundles :]
+    ) = refs[groups + 6 * bundles :]
     rep = rep_ref[0]
     oth = 1 - rep
     side = x_ref.shape[2]
@@ -296,6 +311,9 @@
         v_ref[at:more, :] = v_in[...]
         count = count + count_in[...]
         at = more
+    count = count + gather_rows(blocks, x_ref, y_ref, at)
+    v_ref[at:, :] = dot(y_ref[at:, :], g_ref[0]).astype(BF16)
+    mix_rows(x_ref, slice(at, x_ref.shape[1]), a_ref, ps_ref, rep, own_ref, part_ref)
     inv = 1.0 / count
     inv_ref[...] = inv
     inv = inv[:1, :1]
@@ -316,12 +334,11 @@
     writes.append(write)
 
     xo_ref[...] = x_ref[oth, :, AHEAD:]
-    for c in range((side + AHEAD) // TILE):
-        cols = slice(c * TILE, (c + 1) * TILE)
-        ubuf[cols, :] = (dot_tn(own_ref[:, cols], v_ref[...]) * inv).astype(BF16)
-        to = rep * side + c * TILE if c * TILE < side else oth * side + c * TILE - side
+    for n, (c0, c1) in enumerate(tiles(0, side) + tiles(side, side + AHEAD)):
+        ubuf[c0:c1, :] = (dot_tn(own_ref[:, c0:c1], v_ref[...]) * inv).astype(BF16)
+        to = rep * side + c0 if c0 < side else oth * side + c0 - side
         write = pltpu.make_async_copy(
-            ubuf.at[pl.ds(c * TILE, TILE)], u_out.at[0, pl.ds(to, TILE), :], u_sem.at[c]
+            ubuf.at[pl.ds(c0, c1 - c0)], u_out.at[0, pl.ds(to, c1 - c0), :], u_sem.at[n]
         )
         write.start()
         writes.append(write)
@@ -329,11 +346,12 @@
         write.wait()
 
 
-def products(rep, owner, done, a_shape, hidden):
-    rows = sum(d[1].shape[0] for d in done)
-    _, side, width = a_shape
+def products(rep, owner, groups, done, ps, g_inverse, a_inverse):
+    rows = sum(d[1].shape[0] for d in done) + sum(g.shape[0] for g in groups) * CAP // MAIN
+    _, side, width = a_inverse.shape
+    hidden = g_inverse.shape[1]
     return pl.pallas_call(
-        functools.partial(main_kernel, bundles=len(done)),
+        functools.partial(main_kernel, groups=len(groups), bundles=len(done)),
         name="products",
         out_shape=[
             jax.ShapeDtypeStruct((1, side, width), F32),
@@ -344,7 +362,7 @@
             jax.ShapeDtypeStruct((rows, hidden), BF16),
             jax.ShapeDtypeStruct((8, 128), F32),
         ],
-        in_specs=[SMEM, SMEM] + [VMEM] * (6 * len(done)),
+        in_specs=[SMEM, SMEM] + [VMEM] * (len(groups) + 6 * len(done) + 3),
         out_specs=[ANY, ANY, ANY, VMEM, VMEM, VMEM, VMEM],
         scratch_shapes=[
             pltpu.VMEM((2, rows, side), BF16),
@@ -355,13 +373,13 @@
             pltpu.VMEM((side + AHEAD, hidden), BF16),
             pltpu.SemaphoreType.DMA((side // TILE,)),
             pltpu.SemaphoreType.DMA,
-            pltpu.SemaphoreType.DMA(((side + AHEAD) // TILE,)),
+            pltpu.SemaphoreType.DMA((len(tiles(0, side) + tiles(side, side + AHEAD)),)),
         ],
         compiler_params=pltpu.CompilerParams(vmem_limit_bytes=36 * 2**20),
         cost_estimate=pl.CostEstimate(
             flops=4 * rows * width * side, bytes_accessed=12 * 2**20, transcendentals=0
         ),
-    )(rep, owner, *[value for d in done for value in d])
+    )(rep, owner, *groups, *[value for d in done for value in d], ps, g_inverse, a_inverse)
 
 
 def last_kernel(rep_ref, square_ref, part_ref, x_ref, v_ref, inv_ref, u_in, u_out, ubuf, u_sem):
@@ -370,19 +388,17 @@
     side = 2 * half
     inv = inv_ref[:1, :1]
     stores = []
-    for c in range((half + rest) // TILE):
-        cols = slice(c * TILE, (c + 1) * TILE)
-        at = c * TILE - rest
-        if at < 0:
-            extra = dot_nt(x_ref[:, rest:], square_ref[cols, :])
+    for n, (c0, c1) in enumerate(tiles(rest, rest + half) + tiles(0, rest)):
+        if c0 < rest:
+            extra = dot_nt(x_ref[:, rest:], square_ref[c0:c1, :])
         else:
-            extra = dot(x_ref[:, :rest], square_ref[:, at : at + TILE])
-        mixed = (part_ref[:, cols] + extra).astype(BF16)
-        ubuf[cols, :] = (dot_tn(mixed, v_ref[...]) * inv).astype(BF16)
+            extra = dot(x_ref[:, :rest], square_ref[:, c0 - rest : c1 - rest])
+        mixed = (part_ref[:, c0:c1] + extra).astype(BF16)
+        ubuf[c0:c1, :] = (dot_tn(mixed, v_ref[...]) * inv).astype(BF16)
         store = pltpu.make_async_copy(
-            ubuf.at[pl.ds(c * TILE, TILE)],
-            u_out.at[0, pl.ds(oth * side + half - rest + c * TILE, TILE), :],
-            u_sem.at[c],
+            ubuf.at[pl.ds(c0, c1 - c0)],
+            u_out.at[0, pl.ds(oth * side + half - rest + c0, c1 - c0), :],
+            u_sem.at[n],
         )
         store.start()
         stores.append(store)
@@ -401,7 +417,7 @@
         input_output_aliases={6: 0},
         scratch_shapes=[
             pltpu.VMEM((side, hidden), BF16),
-            pltpu.SemaphoreType.DMA((side // TILE,)),
+            pltpu.SemaphoreType.DMA((side // TILE + 2,)),
         ],
         compiler_params=pltpu.CompilerParams(vmem_limit_bytes=16 * 2**20),
         cost_estimate=pl.CostEstimate(
@@ -432,7 +448,8 @@
     def trade(value, to):
         return lax.ppermute(value, "expert", [(i, to(i)) for i in range(experts)])
 
-    tri = swap(fold(rep, a_inverse))
+    tri = fold(rep, a_inverse)
+    tri = swap(tri)
     mine = (routes.T, tokens, cotangents)
     other = tuple(trade(value, lambda i: i ^ 1) for value in mine)
     blocks = pack(me, mine, other, experts // 2)
@@ -445,10 +462,7 @@
     square = swap(square)
     *first, ps = early(rep, groups, tri, g_inverse, a_inverse, True)
     second = early(rep, others[:3], ps, g_inverse, a_inverse, False)
-    third = early(rep, others[3:], ps, g_inverse, a_inverse, False)
-    a_factor, kept, u, part, xo, v, inv = products(
-        rep, owner, (first, second, third), a_inverse.shape, g_inverse.shape[1]
-    )
+    a_factor, kept, u, part, xo, v, inv = products(rep, owner, others[3:], (first, second), ps, g_inverse, a_inverse)
     return a_factor, kept, finish(rep, square, part, xo, v, inv, u)
 
 

time: 69.8 us -> 62.5 us (0.90)
  the two profiles are of different devices: /device:TPU:24 before, /device:TPU:0 now
where the time goes in v2:
time: 62.5 us; the launch traced here: 62.4 us
  starting transfers between devices  21.6 us (35%)
  waiting for transfers between devices  19.4 us (31%)
  Pallas kernels  17.4 us (28%)
  local copies, waits for them, and re-layouts  2.31 us (4%)
  between operations  1.6 us (3%)
    ppermute x10, starting transfers between devices, trade(): return lax.ppermute(value, 'expert', [(i, to(i)) for i in range(experts)])  14.1 us
    ppermute x10, waiting for transfers between devices, trade(): return lax.ppermute(value, 'expert', [(i, to(i)) for i in range(experts)])  12.9 us
    pallas_call x1, Pallas kernels, products(): pl.pallas_call(functools.partial(main_kernel, groups=len(groups), bundles...  7.48 us
    ppermute x6, starting transfers between devices, swap(): return lax.ppermute(value, 'replica', [(0, 1), (1, 0)])  7.47 us
    ppermute x6, waiting for transfers between devices, swap(): return lax.ppermute(value, 'replica', [(0, 1), (1, 0)])  6.45 us
    pallas_call x2, Pallas kernels, early(): pl.pallas_call(functools.partial(early_kernel, groups=len(groups), unfold...  4.23 us
    pallas_call x1, Pallas kernels, finish(): pl.pallas_call(last_kernel, name='finish', out_shape=jax.ShapeDtypeStruct...  3.1 us
    unnamed x16, local copies, waits for them, and re-layouts  2.25 us
  transfers between devices with their start and end apart: 16, of which 6 were waited for; matrix products, arithmetic and copies ran while one was open for 0% of the time, Pallas kernels for 23%

profile of v2, /device:TPU:0, one launch (start us, length us, event | category | flops | bytes accessed | tf_op | source)
XLA Modules:
  0.0 62.4 jit_solution(11464863998765894708)
XLA Ops:
  0.6 0.0 copy-start.3
  0.6 0.0 copy-start.4
  0.7 0.0 copy-start.5
  0.7 0.6 collective-permute-start.1
  1.2 0.1 collective-permute-start.2
  1.3 0.4 collective-permute-start
  1.7 1.5 %fold.1 = bf16[648,512]{1,0:T(8,128)(2,1)S(1)} custom-call(s32[1]{0:T(128)} %bitcast.rep_ref, bf16[1,1024,2048]{2,1,0:T(8,128)(2,1)} %q_ref.1), custom_call_target="tpu_custom_call" | custom-call | flops 262144 | bytes 1572864 | tf_op jit(solution)/shard_map/fold/pallas_call | solution.py:149
  3.2 2.6 %collective-permute-start.11 = (bf16[648,512]{1,0:T(8,128)(2,1)S(1)}, bf16[648,512]{1,0:T(8,128)(2,1)S(1)}, u32[]{:S(2)}, u32[]{:S(2)}) collective-permute-start(bf16[648,512]{1,0:T(8,128)(2,1)S(1)} %fold.1), channel_id=1, source_target_pairs={{0,1},{1,0},{2,3},{3,2},{4,5},{5,4},{6,7},{7,6},{8,9},{9,8},{10,11... | collective-permute-start | bytes 1990664 | tf_op jit(solution)/shard_map/ppermute | solution.py:446
  5.9 0.0 collective-permute-done.refs_3_
  5.9 0.0 collective-permute-done.2.refs_5_
  5.9 0.0 collective-permute-done.1.refs_4_
  5.9 0.0 copy-done.3
  5.9 0.0 copy-done.4
  5.9 0.0 copy-done.5
  5.9 1.1 %pack.1 = (bf16[16,4224]{1,0:T(8,128)(2,1)S(1)}, bf16[16,4224]{1,0:T(8,128)(2,1)S(1)}, bf16[16,4224]{1,0:T(8,128)(2,1)S(1)}, bf16[16,4224]{1,0:T(8,128)(2,1)S(1)...) custom-call(s32[1]{0:T(128)} %bitcast.1.me_ref, ...), custom_call_target="tpu_custom_call" | custom-call | flops 276824064 | bytes 3145728 | tf_op jit(solution)/shard_map/pack/pallas_call | solution.py:109
  7.0 2.6 %collective-permute-start.9 = (bf16[16,4224]{1,0:T(8,128)(2,1)S(1)}, bf16[16,4224]{1,0:T(8,128)(2,1)S(1)}, u32[]{:S(2)}, u32[]{:S(2)}) collective-permute-start(bf16[16,4224]{1,0:T(8,128)(2,1)S(1)} %get-tuple-element.37), channel_id=1, source_target_pairs={{0,12},{2,14},{4,8},{6,10},{8,20},{10,22},{12,16},{14,18},{16,28},... | collective-permute-start | bytes 405512 | tf_op jit(solution)/shard_map/ppermute | solution.py:449
  9.6 2.2 %collective-permute-start.10 = (bf16[16,4224]{1,0:T(8,128)(2,1)S(1)}, bf16[16,4224]{1,0:T(8,128)(2,1)S(1)}, u32[]{:S(2)}, u32[]{:S(2)}) collective-permute-start(bf16[16,4224]{1,0:T(8,128)(2,1)S(1)} %get-tuple-element.38), channel_id=1, source_target_pairs={{0,28},{2,30},{4,24},{6,26},{8,4},{10,6},{12,0},{14,2},{16,12},{18... | collective-permute-start | bytes 405512 | tf_op jit(solution)/shard_map/ppermute | solution.py:449
  11.8 0.0 collective-permute-start.7
  11.8 3.8 %collective-permute-start.8 = (bf16[16,4224]{1,0:T(8,128)(2,1)S(1)}, bf16[16,4224]{1,0:T(8,128)(2,1)S(1)}, u32[]{:S(2)}, u32[]{:S(2)}) collective-permute-start(bf16[16,4224]{1,0:T(8,128)(2,1)S(1)} %get-tuple-element.36), channel_id=1, source_target_pairs={{0,24},{2,26},{4,28},{6,30},{8,0},{10,2},{12,4},{14,6},{16,8},{18,... | collective-permute-start | bytes 405512 | tf_op jit(solution)/shard_map/ppermute | solution.py:449
  15.6 0.4 collective-permute-done.9
  16.1 1.7 %collective-permute-start.6 = (bf16[16,4224]{1,0:T(8,128)(2,1)S(1)}, bf16[16,4224]{1,0:T(8,128)(2,1)S(1)}, u32[]{:S(2)}, u32[]{:S(2)}) collective-permute-start(bf16[16,4224]{1,0:T(8,128)(2,1)S(1)} %get-tuple-element.34), channel_id=1, source_target_pairs={{0,4},{2,6},{4,0},{6,2},{8,12},{10,14},{12,8},{14,10},{16,20},{18,... | collective-permute-start | bytes 405512 | tf_op jit(solution)/shard_map/ppermute | solution.py:449
  17.8 0.0 copy-start.2
  17.8 4.4 %collective-permute-done.7 = bf16[16,4224]{1,0:T(8,128)(2,1)S(1)} collective-permute-done((bf16[16,4224]{1,0:T(8,128)(2,1)S(1)}, bf16[16,4224]{1,0:T(8,128)(2,1)S(1)}, u32[]{:S(2)}, u32[]{:S(2)}) %collective-permute-start.7) | collective-permute-done | bytes 135200 | tf_op jit(solution)/shard_map/ppermute | solution.py:449
  22.1 0.7 %collective-permute-start.3 = (bf16[16,4224]{1,0:T(8,128)(2,1)S(1)}, bf16[16,4224]{1,0:T(8,128)(2,1)S(1)}, u32[]{:S(2)}, u32[]{:S(2)}) collective-permute-start(bf16[16,4224]{1,0:T(8,128)(2,1)S(1)} %get-tuple-element.31), channel_id=1, source_target_pairs={{0,16},{2,18},{4,20},{6,22},{8,24},{10,26},{12,28},{14,30},{16,0},... | collective-permute-start | bytes 405512 | tf_op jit(solution)/shard_map/ppermute | solution.py:449
  22.9 0.0 collective-permute-done.10
  22.9 2.1 %collective-permute-start.4 = (bf16[16,4224]{1,0:T(8,128)(2,1)S(1)}, bf16[16,4224]{1,0:T(8,128)(2,1)S(1)}, u32[]{:S(2)}, u32[]{:S(2)}) collective-permute-start(bf16[16,4224]{1,0:T(8,128)(2,1)S(1)} %get-tuple-element.32), channel_id=1, source_target_pairs={{0,20},{2,22},{4,16},{6,18},{8,28},{10,30},{12,24},{14,26},{16,4},... | collective-permute-start | bytes 405512 | tf_op jit(solution)/shard_map/ppermute | solution.py:449
  25.0 0.0 collective-permute-done.8
  25.0 0.6 collective-permute-start.14
  25.6 0.0 collective-permute-done.6
  25.6 1.6 %collective-permute-start.13 = (bf16[32,4224]{1,0:T(8,128)(2,1)S(1)}, bf16[32,4224]{1,0:T(8,128)(2,1)S(1)}, u32[]{:S(2)}, u32[]{:S(2)}) collective-permute-start(bf16[32,4224]{1,0:T(8,128)(2,1)S(1)} %constant_dynamic-update-slice_fusion.4.refs_1_), channel_id=1, source_target_pairs={{0,1},{1,0},{2,3},{3,2},{4,5},{5,4},{6,7},{7,6},{8,9},{9,8},{10,11... | collective-permute-start | bytes 811016 | tf_op jit(solution)/shard_map/ppermute | solution.py:446
  27.2 6.7 %collective-permute-done.3 = bf16[16,4224]{1,0:T(8,128)(2,1)S(1)} collective-permute-done((bf16[16,4224]{1,0:T(8,128)(2,1)S(1)}, bf16[16,4224]{1,0:T(8,128)(2,1)S(1)}, u32[]{:S(2)}, u32[]{:S(2)}) %collective-permute-start.3) | collective-permute-done | bytes 135200 | tf_op jit(solution)/shard_map/ppermute | solution.py:449
  33.8 0.5 collective-permute-start.12
  34.4 1.4 %collective-permute-done.4 = bf16[16,4224]{1,0:T(8,128)(2,1)S(1)} collective-permute-done((bf16[16,4224]{1,0:T(8,128)(2,1)S(1)}, bf16[16,4224]{1,0:T(8,128)(2,1)S(1)}, u32[]{:S(2)}, u32[]{:S(2)}) %collective-permute-start.4) | collective-permute-done | bytes 135200 | tf_op jit(solution)/shard_map/ppermute | solution.py:449
  35.9 0.6 collective-permute-start.5
  36.5 2.2 %copy-done = bf16[1,1024,2048]{2,1,0:T(8,128)(2,1)S(1)} copy-done((bf16[1,1024,2048]{2,1,0:T(8,128)(2,1)S(1)}, bf16[1,1024,2048]{2,1,0:T(8,128)(2,1)}, u32[]{:S(2)}) %copy-start) | copy-done | bytes 4194328
  39.5 0.0 collective-permute-done.11.refs_4_
  39.5 1.6 %collective-permute-start.15 = (bf16[384,512]{1,0:T(8,128)(2,1)S(1)}, bf16[384,512]{1,0:T(8,128)(2,1)S(1)}, u32[]{:S(2)}, u32[]{:S(2)}) collective-permute-start(bf16[384,512]{1,0:T(8,128)(2,1)S(1)} %square.1), channel_id=1, source_target_pairs={{0,1},{1,0},{2,3},{3,2},{4,5},{5,4},{6,7},{7,6},{8,9},{9,8},{10,11... | collective-permute-start | bytes 1179656 | tf_op jit(solution)/shard_map/ppermute | solution.py:446
  41.0 0.0 copy-done.2
  41.1 0.0 copy-done.1
  41.1 2.4 %early.2 = (bf16[2,192,1024]{2,1,0:T(8,128)(2,1)S(1)}, bf16[192,768]{1,0:T(8,128)(2,1)S(1)}, bf16[192,1152]{1,0:T(8,128)(2,1)S(1)}, f32[192,896]{1,0:T(8,128)S(1...) custom-call(s32[1]{0:T(128)} %bitcast.rep_ref, ...), custom_call_target="tpu_custom_call" | custom-call | flops 1610612736 | bytes 8388608 | tf_op jit(solution)/shard_map/early/pallas_call | solution.py:273
  43.4 0.0 collective-permute-done.14.refs_2_
  43.5 0.0 collective-permute-done.13.refs_1_
  43.5 2.5 %collective-permute-done.12.refs_0_ = bf16[32,4224]{1,0:T(8,128)(2,1)S(1)} collective-permute-done((bf16[32,4224]{1,0:T(8,128)(2,1)S(1)}, bf16[32,4224]{1,0:T(8,128)(2,1)S(1)}, u32[]{:S(2)}, u32[]{:S(2)}) %collective-permute-start.12) | collective-permute-done | bytes 270368 | tf_op jit(solution)/shard_map/ppermute | solution.py:446
  46.0 1.8 %early.3 = (bf16[2,144,1024]{2,1,0:T(8,128)(2,1)S(1)}, bf16[144,768]{1,0:T(8,128)(2,1)S(1)}, bf16[144,1152]{1,0:T(8,128)(2,1)S(1)}, f32[144,896]{1,0:T(8,128)S(1...) custom-call(s32[1]{0:T(128)} %bitcast.rep_ref, bf16[32,4224]{1,0:T(8,128)(2,1)S(1)} %collective-permute-done.12.refs_0_, ...), custom_call_target="tpu_custom_call" | custom-call | flops 1207959552 | bytes 8388608 | tf_op jit(solution)/shard_map/early/pallas_call | solution.py:273
  47.8 3.9 %collective-permute-done.5.refs_0_ = bf16[32,4224]{1,0:T(8,128)(2,1)S(1)} collective-permute-done((bf16[32,4224]{1,0:T(8,128)(2,1)S(1)}, bf16[32,4224]{1,0:T(8,128)(2,1)S(1)}, u32[]{:S(2)}, u32[]{:S(2)}) %collective-permute-start.5) | collective-permute-done | bytes 270368 | tf_op jit(solution)/shard_map/ppermute | solution.py:446
  51.8 7.5 %products.1 = (f32[1,1024,2048]{2,1,0:T(8,128)}, f32[1,1,768,768]{3,2,1,0:T(8,128)}, bf16[1,2048,768]{2,1,0:T(8,128)(2,1)}, f32[384,896]{1,0:T(8,128)S(1)}, bf16...) custom-call(s32[1]{0:T(128)} %bitcast.rep_ref, s32[1]{0:T(128)S(6)} %copy.15.owner_ref, ...), custom_call_target="tpu_custom_call" | custom-call | flops 3221225472 | bytes 12582912 | tf_op jit(solution)/shard_map/products/pallas_call | solution.py:353
  59.2 0.0 collective-permute-done.15.square_ref
  59.3 3.1 %finish.1 = bf16[1,2048,768]{2,1,0:T(8,128)(2,1)} custom-call(s32[1]{0:T(128)} %bitcast.rep_ref, bf16[384,512]{1,0:T(8,128)(2,1)S(1)} %collective-permute-done.15.square_ref, f32[384,896]{1,0:T(8,128)S(1)} %get-tuple-element.54.part_ref, bf16[384,896]{1,0:T(8,128)(2,1)S(1)} %get-tuple-element.55.x_ref, ...), custom_call_target="tpu_custom_call", output_to_operand_aliasing={{}: (6, {})} | custom-call | flops 1145044992 | bytes 4194304 | tf_op jit(solution)/shard_map/finish/pallas_call | solution.py:411
  (11 shorter events, 0.1 us)
Async XLA Ops:
  0.6 5.2 %copy-start.3 = (bf16[128,2048]{1,0:T(8,128)(2,1)S(1)}, bf16[128,2048]{1,0:T(8,128)(2,1)}, u32[]{:S(2)}) copy-start(bf16[128,2048]{1,0:T(8,128)(2,1)} %refs_1_.1) | copy-start | bytes 1572868
  0.6 5.2 %copy-start.4 = (bf16[128,768]{1,0:T(8,128)(2,1)S(1)}, bf16[128,768]{1,0:T(8,128)(2,1)}, u32[]{:S(2)}) copy-start(bf16[128,768]{1,0:T(8,128)(2,1)} %refs_2_.1) | copy-start | bytes 589828
  0.7 5.2 %copy-start.5 = (s32[128,8]{0,1:T(8,128)S(1)}, s32[128,8]{0,1:T(8,128)}, u32[]{:S(2)}) copy-start(s32[128,8]{0,1:T(8,128)} %param.8) | copy-start | bytes 12292
  0.7 5.2 %collective-permute-start.1 = (bf16[128,2048]{1,0:T(8,128)(2,1)}, bf16[128,2048]{1,0:T(8,128)(2,1)S(1)}, u32[]{:S(2)}, u32[]{:S(2)}) collective-permute-start(bf16[128,2048]{1,0:T(8,128)(2,1)} %refs_1_.1), channel_id=1, source_target_pairs={{0,2},{2,0},{4,6},{6,4},{8,10},{10,8},{12,14},{14,12},{16,18},{18,... | collective-permute-start | bytes 1572872 | tf_op jit(solution)/shard_map/ppermute | solution.py:449
  1.2 4.7 %collective-permute-start.2 = (bf16[128,768]{1,0:T(8,128)(2,1)}, bf16[128,768]{1,0:T(8,128)(2,1)S(1)}, u32[]{:S(2)}, u32[]{:S(2)}) collective-permute-start(bf16[128,768]{1,0:T(8,128)(2,1)} %refs_2_.1), channel_id=1, source_target_pairs={{0,2},{2,0},{4,6},{6,4},{8,10},{10,8},{12,14},{14,12},{16,18},{18,... | collective-permute-start | bytes 589832 | tf_op jit(solution)/shard_map/ppermute | solution.py:449
  1.3 4.6 %collective-permute-start = (s32[8,128]{1,0:T(8,128)}, s32[8,128]{1,0:T(8,128)S(1)}, u32[]{:S(2)}, u32[]{:S(2)}) collective-permute-start(s32[8,128]{1,0:T(8,128)} %bitcast.3), channel_id=1, source_target_pairs={{0,2},{2,0},{4,6},{6,4},{8,10},{10,8},{12,14},{14,12},{16,18},{18,... | collective-permute-start | bytes 12296 | tf_op jit(solution)/shard_map/ppermute | solution.py:449
  3.2 36.2 %collective-permute-start.11 = (bf16[648,512]{1,0:T(8,128)(2,1)S(1)}, bf16[648,512]{1,0:T(8,128)(2,1)S(1)}, u32[]{:S(2)}, u32[]{:S(2)}) collective-permute-start(bf16[648,512]{1,0:T(8,128)(2,1)S(1)} %fold.1), channel_id=1, source_target_pairs={{0,1},{1,0},{2,3},{3,2},{4,5},{5,4},{6,7},{7,6},{8,9},{9,8},{10,11... | collective-permute-start | bytes 1990664 | tf_op jit(solution)/shard_map/ppermute | solution.py:446
  7.0 9.1 %collective-permute-start.9 = (bf16[16,4224]{1,0:T(8,128)(2,1)S(1)}, bf16[16,4224]{1,0:T(8,128)(2,1)S(1)}, u32[]{:S(2)}, u32[]{:S(2)}) collective-permute-start(bf16[16,4224]{1,0:T(8,128)(2,1)S(1)} %get-tuple-element.37), channel_id=1, source_target_pairs={{0,12},{2,14},{4,8},{6,10},{8,20},{10,22},{12,16},{14,18},{16,28},... | collective-permute-start | bytes 405512 | tf_op jit(solution)/shard_map/ppermute | solution.py:449
  9.6 13.3 %collective-permute-start.10 = (bf16[16,4224]{1,0:T(8,128)(2,1)S(1)}, bf16[16,4224]{1,0:T(8,128)(2,1)S(1)}, u32[]{:S(2)}, u32[]{:S(2)}) collective-permute-start(bf16[16,4224]{1,0:T(8,128)(2,1)S(1)} %get-tuple-element.38), channel_id=1, source_target_pairs={{0,28},{2,30},{4,24},{6,26},{8,4},{10,6},{12,0},{14,2},{16,12},{18... | collective-permute-start | bytes 405512 | tf_op jit(solution)/shard_map/ppermute | solution.py:449
  11.8 10.4 %collective-permute-start.7 = (bf16[16,4224]{1,0:T(8,128)(2,1)S(1)}, bf16[16,4224]{1,0:T(8,128)(2,1)S(1)}, u32[]{:S(2)}, u32[]{:S(2)}) collective-permute-start(bf16[16,4224]{1,0:T(8,128)(2,1)S(1)} %get-tuple-element.35), channel_id=1, source_target_pairs={{0,8},{2,10},{4,12},{6,14},{8,16},{10,18},{12,20},{14,22},{16,24},... | collective-permute-start | bytes 405512 | tf_op jit(solution)/shard_map/ppermute | solution.py:449
  11.8 13.2 %collective-permute-start.8 = (bf16[16,4224]{1,0:T(8,128)(2,1)S(1)}, bf16[16,4224]{1,0:T(8,128)(2,1)S(1)}, u32[]{:S(2)}, u32[]{:S(2)}) collective-permute-start(bf16[16,4224]{1,0:T(8,128)(2,1)S(1)} %get-tuple-element.36), channel_id=1, source_target_pairs={{0,24},{2,26},{4,28},{6,30},{8,0},{10,2},{12,4},{14,6},{16,8},{18,... | collective-permute-start | bytes 405512 | tf_op jit(solution)/shard_map/ppermute | solution.py:449
  16.1 9.5 %collective-permute-start.6 = (bf16[16,4224]{1,0:T(8,128)(2,1)S(1)}, bf16[16,4224]{1,0:T(8,128)(2,1)S(1)}, u32[]{:S(2)}, u32[]{:S(2)}) collective-permute-start(bf16[16,4224]{1,0:T(8,128)(2,1)S(1)} %get-tuple-element.34), channel_id=1, source_target_pairs={{0,4},{2,6},{4,0},{6,2},{8,12},{10,14},{12,8},{14,10},{16,20},{18,... | collective-permute-start | bytes 405512 | tf_op jit(solution)/shard_map/ppermute | solution.py:449
  17.8 23.3 %copy-start.2 = (bf16[1,768,768]{2,1,0:T(8,128)(2,1)S(1)}, bf16[1,768,768]{2,1,0:T(8,128)(2,1)}, u32[]{:S(2)}) copy-start(bf16[1,768,768]{2,1,0:T(8,128)(2,1)} %refs_14_.1) | copy-start | bytes 3538948
  22.1 11.7 %collective-permute-start.3 = (bf16[16,4224]{1,0:T(8,128)(2,1)S(1)}, bf16[16,4224]{1,0:T(8,128)(2,1)S(1)}, u32[]{:S(2)}, u32[]{:S(2)}) collective-permute-start(bf16[16,4224]{1,0:T(8,128)(2,1)S(1)} %get-tuple-element.31), channel_id=1, source_target_pairs={{0,16},{2,18},{4,20},{6,22},{8,24},{10,26},{12,28},{14,30},{16,0},... | collective-permute-start | bytes 405512 | tf_op jit(solution)/shard_map/ppermute | solution.py:449
  22.9 13.0 %collective-permute-start.4 = (bf16[16,4224]{1,0:T(8,128)(2,1)S(1)}, bf16[16,4224]{1,0:T(8,128)(2,1)S(1)}, u32[]{:S(2)}, u32[]{:S(2)}) collective-permute-start(bf16[16,4224]{1,0:T(8,128)(2,1)S(1)} %get-tuple-element.32), channel_id=1, source_target_pairs={{0,20},{2,22},{4,16},{6,18},{8,28},{10,30},{12,24},{14,26},{16,4},... | collective-permute-start | bytes 405512 | tf_op jit(solution)/shard_map/ppermute | solution.py:449
  25.0 18.5 %collective-permute-start.14 = (bf16[32,4224]{1,0:T(8,128)(2,1)S(1)}, bf16[32,4224]{1,0:T(8,128)(2,1)S(1)}, u32[]{:S(2)}, u32[]{:S(2)}) collective-permute-start(bf16[32,4224]{1,0:T(8,128)(2,1)S(1)} %constant_dynamic-update-slice_fusion.6.refs_2_), channel_id=1, source_target_pairs={{0,1},{1,0},{2,3},{3,2},{4,5},{5,4},{6,7},{7,6},{8,9},{9,8},{10,11... | collective-permute-start | bytes 811016 | tf_op jit(solution)/shard_map/ppermute | solution.py:446
  25.6 17.9 %collective-permute-start.13 = (bf16[32,4224]{1,0:T(8,128)(2,1)S(1)}, bf16[32,4224]{1,0:T(8,128)(2,1)S(1)}, u32[]{:S(2)}, u32[]{:S(2)}) collective-permute-start(bf16[32,4224]{1,0:T(8,128)(2,1)S(1)} %constant_dynamic-update-slice_fusion.4.refs_1_), channel_id=1, source_target_pairs={{0,1},{1,0},{2,3},{3,2},{4,5},{5,4},{6,7},{7,6},{8,9},{9,8},{10,11... | collective-permute-start | bytes 811016 | tf_op jit(solution)/shard_map/ppermute | solution.py:446
  33.8 12.1 %collective-permute-start.12 = (bf16[32,4224]{1,0:T(8,128)(2,1)S(1)}, bf16[32,4224]{1,0:T(8,128)(2,1)S(1)}, u32[]{:S(2)}, u32[]{:S(2)}) collective-permute-start(bf16[32,4224]{1,0:T(8,128)(2,1)S(1)} %constant_dynamic-update-slice_fusion.2.refs_0_), channel_id=1, source_target_pairs={{0,1},{1,0},{2,3},{3,2},{4,5},{5,4},{6,7},{7,6},{8,9},{9,8},{10,11... | collective-permute-start | bytes 811016 | tf_op jit(solution)/shard_map/ppermute | solution.py:446
  35.9 15.9 %collective-permute-start.5 = (bf16[32,4224]{1,0:T(8,128)(2,1)S(1)}, bf16[32,4224]{1,0:T(8,128)(2,1)S(1)}, u32[]{:S(2)}, u32[]{:S(2)}) collective-permute-start(bf16[32,4224]{1,0:T(8,128)(2,1)S(1)} %constant_dynamic-update-slice_fusion.refs_3_), channel_id=1, source_target_pairs={{0,1},{1,0},{2,3},{3,2},{4,5},{5,4},{6,7},{7,6},{8,9},{9,8},{10,11... | collective-permute-start | bytes 811016 | tf_op jit(solution)/shard_map/ppermute | solution.py:446
  36.5 2.2 %copy-start = (bf16[1,1024,2048]{2,1,0:T(8,128)(2,1)S(1)}, bf16[1,1024,2048]{2,1,0:T(8,128)(2,1)}, u32[]{:S(2)}) copy-start(bf16[1,1024,2048]{2,1,0:T(8,128)(2,1)} %q_ref.1) | copy-start | bytes 12582916
  38.6 2.4 %copy-start.1 = (bf16[1,1024,2048]{2,1,0:T(8,128)(2,1)S(1)}, bf16[1,1024,2048]{2,1,0:T(8,128)(2,1)}, u32[]{:S(2)}) copy-start(bf16[1,1024,2048]{2,1,0:T(8,128)(2,1)} %q_ref.1) | copy-start | bytes 12582916
  39.5 19.8 %collective-permute-start.15 = (bf16[384,512]{1,0:T(8,128)(2,1)S(1)}, bf16[384,512]{1,0:T(8,128)(2,1)S(1)}, u32[]{:S(2)}, u32[]{:S(2)}) collective-permute-start(bf16[384,512]{1,0:T(8,128)(2,1)S(1)} %square.1), channel_id=1, source_target_pairs={{0,1},{1,0},{2,3},{3,2},{4,5},{5,4},{6,7},{7,6},{8,9},{9,8},{10,11... | collective-permute-start | bytes 1179656 | tf_op jit(solution)/shard_map/ppermute | solution.py:446

commit v3 on v2

--- a/solution.py
+++ b/solution.py
@@ -334,7 +334,7 @@
     writes.append(write)
 
     xo_ref[...] = x_ref[oth, :, AHEAD:]
-    for n, (c0, c1) in enumerate(tiles(0, side) + tiles(side, side + AHEAD)):
+    for n, (c0, c1) in enumerate([(0, side // 2), (side // 2, side)] + tiles(side, side + AHEAD)):
         ubuf[c0:c1, :] = (dot_tn(own_ref[:, c0:c1], v_ref[...]) * inv).astype(BF16)
         to = rep * side + c0 if c0 < side else oth * side + c0 - side
         write = pltpu.make_async_copy(
@@ -388,7 +388,7 @@
     side = 2 * half
     inv = inv_ref[:1, :1]
     stores = []
-    for n, (c0, c1) in enumerate(tiles(rest, rest + half) + tiles(0, rest)):
+    for n, (c0, c1) in enumerate([(rest, rest + half), (0, rest)]):
         if c0 < rest:
             extra = dot_nt(x_ref[:, rest:], square_ref[c0:c1, :])
         else:
@@ -417,7 +417,7 @@
         input_output_aliases={6: 0},
         scratch_shapes=[
             pltpu.VMEM((side, hidden), BF16),
-            pltpu.SemaphoreType.DMA((side // TILE + 2,)),
+            pltpu.SemaphoreType.DMA((2,)),
         ],
         compiler_params=pltpu.CompilerParams(vmem_limit_bytes=16 * 2**20),
         cost_estimate=pl.CostEstimate(

time: 62.5 us -> 61.9 us (level)
  no operation moved by 1% of the time
where the time goes in v3:
time: 61.9 us; the launch traced here: 61.7 us
  starting transfers between devices  21.6 us (35%)
  waiting for transfers between devices  19.4 us (31%)
  Pallas kernels  16.8 us (27%)
  local copies, waits for them, and re-layouts  2.31 us (4%)
  between operations  1.6 us (3%)
    ppermute x10, starting transfers between devices, trade(): return lax.ppermute(value, 'expert', [(i, to(i)) for i in range(experts)])  14.1 us
    ppermute x10, waiting for transfers between devices, trade(): return lax.ppermute(value, 'expert', [(i, to(i)) for i in range(experts)])  12.9 us
    ppermute x6, starting transfers between devices, swap(): return lax.ppermute(value, 'replica', [(0, 1), (1, 0)])  7.47 us
    pallas_call x1, Pallas kernels, products(): pl.pallas_call(functools.partial(main_kernel, groups=len(groups), bundles...  7.36 us
    ppermute x6, waiting for transfers between devices, swap(): return lax.ppermute(value, 'replica', [(0, 1), (1, 0)])  6.45 us
    pallas_call x2, Pallas kernels, early(): pl.pallas_call(functools.partial(early_kernel, groups=len(groups), unfold...  4.23 us
    pallas_call x1, Pallas kernels, finish(): pl.pallas_call(last_kernel, name='finish', out_shape=jax.ShapeDtypeStruct...  2.54 us
    unnamed x16, local copies, waits for them, and re-layouts  2.25 us
  transfers between devices with their start and end apart: 16, of which 6 were waited for; matrix products, arithmetic and copies ran while one was open for 0% of the time, Pallas kernels for 23%

profile of v3, /device:TPU:0, one launch (start us, length us, event | category | flops | bytes accessed | tf_op | source)
XLA Modules:
  0.0 61.7 jit_solution(16883491970452520351)
XLA Ops:
  0.6 0.0 copy-start.3
  0.6 0.0 copy-start.4
  0.7 0.0 copy-start.5
  0.7 0.6 collective-permute-start.1
  1.2 0.1 collective-permute-start.2
  1.3 0.4 collective-permute-start
  1.7 1.5 %fold.1 = bf16[648,512]{1,0:T(8,128)(2,1)S(1)} custom-call(s32[1]{0:T(128)} %bitcast.rep_ref, bf16[1,1024,2048]{2,1,0:T(8,128)(2,1)} %q_ref.1), custom_call_target="tpu_custom_call" | custom-call | flops 262144 | bytes 1572864 | tf_op jit(solution)/shard_map/fold/pallas_call | solution.py:149
  3.2 2.6 %collective-permute-start.11 = (bf16[648,512]{1,0:T(8,128)(2,1)S(1)}, bf16[648,512]{1,0:T(8,128)(2,1)S(1)}, u32[]{:S(2)}, u32[]{:S(2)}) collective-permute-start(bf16[648,512]{1,0:T(8,128)(2,1)S(1)} %fold.1), channel_id=1, source_target_pairs={{0,1},{1,0},{2,3},{3,2},{4,5},{5,4},{6,7},{7,6},{8,9},{9,8},{10,11... | collective-permute-start | bytes 1990664 | tf_op jit(solution)/shard_map/ppermute | solution.py:446
  5.9 0.0 collective-permute-done.refs_3_
  5.9 0.0 collective-permute-done.2.refs_5_
  5.9 0.0 collective-permute-done.1.refs_4_
  5.9 0.0 copy-done.3
  5.9 0.0 copy-done.4
  5.9 0.0 copy-done.5
  5.9 1.1 %pack.1 = (bf16[16,4224]{1,0:T(8,128)(2,1)S(1)}, bf16[16,4224]{1,0:T(8,128)(2,1)S(1)}, bf16[16,4224]{1,0:T(8,128)(2,1)S(1)}, bf16[16,4224]{1,0:T(8,128)(2,1)S(1)...) custom-call(s32[1]{0:T(128)} %bitcast.1.me_ref, ...), custom_call_target="tpu_custom_call" | custom-call | flops 276824064 | bytes 3145728 | tf_op jit(solution)/shard_map/pack/pallas_call | solution.py:109
  7.0 2.6 %collective-permute-start.9 = (bf16[16,4224]{1,0:T(8,128)(2,1)S(1)}, bf16[16,4224]{1,0:T(8,128)(2,1)S(1)}, u32[]{:S(2)}, u32[]{:S(2)}) collective-permute-start(bf16[16,4224]{1,0:T(8,128)(2,1)S(1)} %get-tuple-element.37), channel_id=1, source_target_pairs={{0,12},{2,14},{4,8},{6,10},{8,20},{10,22},{12,16},{14,18},{16,28},... | collective-permute-start | bytes 405512 | tf_op jit(solution)/shard_map/ppermute | solution.py:449
  9.6 2.2 %collective-permute-start.10 = (bf16[16,4224]{1,0:T(8,128)(2,1)S(1)}, bf16[16,4224]{1,0:T(8,128)(2,1)S(1)}, u32[]{:S(2)}, u32[]{:S(2)}) collective-permute-start(bf16[16,4224]{1,0:T(8,128)(2,1)S(1)} %get-tuple-element.38), channel_id=1, source_target_pairs={{0,28},{2,30},{4,24},{6,26},{8,4},{10,6},{12,0},{14,2},{16,12},{18... | collective-permute-start | bytes 405512 | tf_op jit(solution)/shard_map/ppermute | solution.py:449
  11.8 0.0 collective-permute-start.7
  11.8 3.8 %collective-permute-start.8 = (bf16[16,4224]{1,0:T(8,128)(2,1)S(1)}, bf16[16,4224]{1,0:T(8,128)(2,1)S(1)}, u32[]{:S(2)}, u32[]{:S(2)}) collective-permute-start(bf16[16,4224]{1,0:T(8,128)(2,1)S(1)} %get-tuple-element.36), channel_id=1, source_target_pairs={{0,24},{2,26},{4,28},{6,30},{8,0},{10,2},{12,4},{14,6},{16,8},{18,... | collective-permute-start | bytes 405512 | tf_op jit(solution)/shard_map/ppermute | solution.py:449
  15.6 0.4 collective-permute-done.9
  16.1 1.7 %collective-permute-start.6 = (bf16[16,4224]{1,0:T(8,128)(2,1)S(1)}, bf16[16,4224]{1,0:T(8,128)(2,1)S(1)}, u32[]{:S(2)}, u32[]{:S(2)}) collective-permute-start(bf16[16,4224]{1,0:T(8,128)(2,1)S(1)} %get-tuple-element.34), channel_id=1, source_target_pairs={{0,4},{2,6},{4,0},{6,2},{8,12},{10,14},{12,8},{14,10},{16,20},{18,... | collective-permute-start | bytes 405512 | tf_op jit(solution)/shard_map/ppermute | solution.py:449
  17.8 0.0 copy-start.2
  17.8 4.4 %collective-permute-done.7 = bf16[16,4224]{1,0:T(8,128)(2,1)S(1)} collective-permute-done((bf16[16,4224]{1,0:T(8,128)(2,1)S(1)}, bf16[16,4224]{1,0:T(8,128)(2,1)S(1)}, u32[]{:S(2)}, u32[]{:S(2)}) %collective-permute-start.7) | collective-permute-done | bytes 135200 | tf_op jit(solution)/shard_map/ppermute | solution.py:449
  22.1 0.7 %collective-permute-start.3 = (bf16[16,4224]{1,0:T(8,128)(2,1)S(1)}, bf16[16,4224]{1,0:T(8,128)(2,1)S(1)}, u32[]{:S(2)}, u32[]{:S(2)}) collective-permute-start(bf16[16,4224]{1,0:T(8,128)(2,1)S(1)} %get-tuple-element.31), channel_id=1, source_target_pairs={{0,16},{2,18},{4,20},{6,22},{8,24},{10,26},{12,28},{14,30},{16,0},... | collective-permute-start | bytes 405512 | tf_op jit(solution)/shard_map/ppermute | solution.py:449
  22.9 0.0 collective-permute-done.10
  22.9 2.1 %collective-permute-start.4 = (bf16[16,4224]{1,0:T(8,128)(2,1)S(1)}, bf16[16,4224]{1,0:T(8,128)(2,1)S(1)}, u32[]{:S(2)}, u32[]{:S(2)}) collective-permute-start(bf16[16,4224]{1,0:T(8,128)(2,1)S(1)} %get-tuple-element.32), channel_id=1, source_target_pairs={{0,20},{2,22},{4,16},{6,18},{8,28},{10,30},{12,24},{14,26},{16,4},... | collective-permute-start | bytes 405512 | tf_op jit(solution)/shard_map/ppermute | solution.py:449
  25.0 0.0 collective-permute-done.8
  25.0 0.6 collective-permute-start.14
  25.6 0.0 collective-permute-done.6
  25.6 1.6 %collective-permute-start.13 = (bf16[32,4224]{1,0:T(8,128)(2,1)S(1)}, bf16[32,4224]{1,0:T(8,128)(2,1)S(1)}, u32[]{:S(2)}, u32[]{:S(2)}) collective-permute-start(bf16[32,4224]{1,0:T(8,128)(2,1)S(1)} %constant_dynamic-update-slice_fusion.4.refs_1_), channel_id=1, source_target_pairs={{0,1},{1,0},{2,3},{3,2},{4,5},{5,4},{6,7},{7,6},{8,9},{9,8},{10,11... | collective-permute-start | bytes 811016 | tf_op jit(solution)/shard_map/ppermute | solution.py:446
  27.2 6.7 %collective-permute-done.3 = bf16[16,4224]{1,0:T(8,128)(2,1)S(1)} collective-permute-done((bf16[16,4224]{1,0:T(8,128)(2,1)S(1)}, bf16[16,4224]{1,0:T(8,128)(2,1)S(1)}, u32[]{:S(2)}, u32[]{:S(2)}) %collective-permute-start.3) | collective-permute-done | bytes 135200 | tf_op jit(solution)/shard_map/ppermute | solution.py:449
  33.8 0.5 collective-permute-start.12
  34.4 1.4 %collective-permute-done.4 = bf16[16,4224]{1,0:T(8,128)(2,1)S(1)} collective-permute-done((bf16[16,4224]{1,0:T(8,128)(2,1)S(1)}, bf16[16,4224]{1,0:T(8,128)(2,1)S(1)}, u32[]{:S(2)}, u32[]{:S(2)}) %collective-permute-start.4) | collective-permute-done | bytes 135200 | tf_op jit(solution)/shard_map/ppermute | solution.py:449
  35.9 0.6 collective-permute-start.5
  36.5 2.2 %copy-done = bf16[1,1024,2048]{2,1,0:T(8,128)(2,1)S(1)} copy-done((bf16[1,1024,2048]{2,1,0:T(8,128)(2,1)S(1)}, bf16[1,1024,2048]{2,1,0:T(8,128)(2,1)}, u32[]{:S(2)}) %copy-start) | copy-done | bytes 4194328
  39.5 0.0 collective-permute-done.11.refs_4_
  39.5 1.6 %collective-permute-start.15 = (bf16[384,512]{1,0:T(8,128)(2,1)S(1)}, bf16[384,512]{1,0:T(8,128)(2,1)S(1)}, u32[]{:S(2)}, u32[]{:S(2)}) collective-permute-start(bf16[384,512]{1,0:T(8,128)(2,1)S(1)} %square.1), channel_id=1, source_target_pairs={{0,1},{1,0},{2,3},{3,2},{4,5},{5,4},{6,7},{7,6},{8,9},{9,8},{10,11... | collective-permute-start | bytes 1179656 | tf_op jit(solution)/shard_map/ppermute | solution.py:446
  41.0 0.0 copy-done.2
  41.1 0.0 copy-done.1
  41.1 2.4 %early.2 = (bf16[2,192,1024]{2,1,0:T(8,128)(2,1)S(1)}, bf16[192,768]{1,0:T(8,128)(2,1)S(1)}, bf16[192,1152]{1,0:T(8,128)(2,1)S(1)}, f32[192,896]{1,0:T(8,128)S(1...) custom-call(s32[1]{0:T(128)} %bitcast.rep_ref, ...), custom_call_target="tpu_custom_call" | custom-call | flops 1610612736 | bytes 8388608 | tf_op jit(solution)/shard_map/early/pallas_call | solution.py:273
  43.4 0.0 collective-permute-done.14.refs_2_
  43.5 0.0 collective-permute-done.13.refs_1_
  43.5 2.5 %collective-permute-done.12.refs_0_ = bf16[32,4224]{1,0:T(8,128)(2,1)S(1)} collective-permute-done((bf16[32,4224]{1,0:T(8,128)(2,1)S(1)}, bf16[32,4224]{1,0:T(8,128)(2,1)S(1)}, u32[]{:S(2)}, u32[]{:S(2)}) %collective-permute-start.12) | collective-permute-done | bytes 270368 | tf_op jit(solution)/shard_map/ppermute | solution.py:446
  46.0 1.8 %early.3 = (bf16[2,144,1024]{2,1,0:T(8,128)(2,1)S(1)}, bf16[144,768]{1,0:T(8,128)(2,1)S(1)}, bf16[144,1152]{1,0:T(8,128)(2,1)S(1)}, f32[144,896]{1,0:T(8,128)S(1...) custom-call(s32[1]{0:T(128)} %bitcast.rep_ref, bf16[32,4224]{1,0:T(8,128)(2,1)S(1)} %collective-permute-done.12.refs_0_, ...), custom_call_target="tpu_custom_call" | custom-call | flops 1207959552 | bytes 8388608 | tf_op jit(solution)/shard_map/early/pallas_call | solution.py:273
  47.8 3.9 %collective-permute-done.5.refs_0_ = bf16[32,4224]{1,0:T(8,128)(2,1)S(1)} collective-permute-done((bf16[32,4224]{1,0:T(8,128)(2,1)S(1)}, bf16[32,4224]{1,0:T(8,128)(2,1)S(1)}, u32[]{:S(2)}, u32[]{:S(2)}) %collective-permute-start.5) | collective-permute-done | bytes 270368 | tf_op jit(solution)/shard_map/ppermute | solution.py:446
  51.8 7.4 %products.1 = (f32[1,1024,2048]{2,1,0:T(8,128)}, f32[1,1,768,768]{3,2,1,0:T(8,128)}, bf16[1,2048,768]{2,1,0:T(8,128)(2,1)}, f32[384,896]{1,0:T(8,128)S(1)}, bf16...) custom-call(s32[1]{0:T(128)} %bitcast.rep_ref, s32[1]{0:T(128)S(6)} %copy.15.owner_ref, ...), custom_call_target="tpu_custom_call" | custom-call | flops 3221225472 | bytes 12582912 | tf_op jit(solution)/shard_map/products/pallas_call | solution.py:353
  59.1 0.0 collective-permute-done.15.square_ref
  59.1 2.5 %finish.1 = bf16[1,2048,768]{2,1,0:T(8,128)(2,1)} custom-call(s32[1]{0:T(128)} %bitcast.rep_ref, bf16[384,512]{1,0:T(8,128)(2,1)S(1)} %collective-permute-done.15.square_ref, f32[384,896]{1,0:T(8,128)S(1)} %get-tuple-element.54.part_ref, bf16[384,896]{1,0:T(8,128)(2,1)S(1)} %get-tuple-element.55.x_ref, ...), custom_call_target="tpu_custom_call", output_to_operand_aliasing={{}: (6, {})} | custom-call | flops 1145044992 | bytes 4194304 | tf_op jit(solution)/shard_map/finish/pallas_call | solution.py:411
  (11 shorter events, 0.1 us)
Async XLA Ops:
  0.6 5.2 %copy-start.3 = (bf16[128,2048]{1,0:T(8,128)(2,1)S(1)}, bf16[128,2048]{1,0:T(8,128)(2,1)}, u32[]{:S(2)}) copy-start(bf16[128,2048]{1,0:T(8,128)(2,1)} %refs_1_.1) | copy-start | bytes 1572868
  0.6 5.2 %copy-start.4 = (bf16[128,768]{1,0:T(8,128)(2,1)S(1)}, bf16[128,768]{1,0:T(8,128)(2,1)}, u32[]{:S(2)}) copy-start(bf16[128,768]{1,0:T(8,128)(2,1)} %refs_2_.1) | copy-start | bytes 589828
  0.7 5.2 %copy-start.5 = (s32[128,8]{0,1:T(8,128)S(1)}, s32[128,8]{0,1:T(8,128)}, u32[]{:S(2)}) copy-start(s32[128,8]{0,1:T(8,128)} %param.8) | copy-start | bytes 12292
  0.7 5.2 %collective-permute-start.1 = (bf16[128,2048]{1,0:T(8,128)(2,1)}, bf16[128,2048]{1,0:T(8,128)(2,1)S(1)}, u32[]{:S(2)}, u32[]{:S(2)}) collective-permute-start(bf16[128,2048]{1,0:T(8,128)(2,1)} %refs_1_.1), channel_id=1, source_target_pairs={{0,2},{2,0},{4,6},{6,4},{8,10},{10,8},{12,14},{14,12},{16,18},{18,... | collective-permute-start | bytes 1572872 | tf_op jit(solution)/shard_map/ppermute | solution.py:449
  1.2 4.7 %collective-permute-start.2 = (bf16[128,768]{1,0:T(8,128)(2,1)}, bf16[128,768]{1,0:T(8,128)(2,1)S(1)}, u32[]{:S(2)}, u32[]{:S(2)}) collective-permute-start(bf16[128,768]{1,0:T(8,128)(2,1)} %refs_2_.1), channel_id=1, source_target_pairs={{0,2},{2,0},{4,6},{6,4},{8,10},{10,8},{12,14},{14,12},{16,18},{18,... | collective-permute-start | bytes 589832 | tf_op jit(solution)/shard_map/ppermute | solution.py:449
  1.3 4.6 %collective-permute-start = (s32[8,128]{1,0:T(8,128)}, s32[8,128]{1,0:T(8,128)S(1)}, u32[]{:S(2)}, u32[]{:S(2)}) collective-permute-start(s32[8,128]{1,0:T(8,128)} %bitcast.3), channel_id=1, source_target_pairs={{0,2},{2,0},{4,6},{6,4},{8,10},{10,8},{12,14},{14,12},{16,18},{18,... | collective-permute-start | bytes 12296 | tf_op jit(solution)/shard_map/ppermute | solution.py:449
  3.2 36.2 %collective-permute-start.11 = (bf16[648,512]{1,0:T(8,128)(2,1)S(1)}, bf16[648,512]{1,0:T(8,128)(2,1)S(1)}, u32[]{:S(2)}, u32[]{:S(2)}) collective-permute-start(bf16[648,512]{1,0:T(8,128)(2,1)S(1)} %fold.1), channel_id=1, source_target_pairs={{0,1},{1,0},{2,3},{3,2},{4,5},{5,4},{6,7},{7,6},{8,9},{9,8},{10,11... | collective-permute-start | bytes 1990664 | tf_op jit(solution)/shard_map/ppermute | solution.py:446
  7.0 9.1 %collective-permute-start.9 = (bf16[16,4224]{1,0:T(8,128)(2,1)S(1)}, bf16[16,4224]{1,0:T(8,128)(2,1)S(1)}, u32[]{:S(2)}, u32[]{:S(2)}) collective-permute-start(bf16[16,4224]{1,0:T(8,128)(2,1)S(1)} %get-tuple-element.37), channel_id=1, source_target_pairs={{0,12},{2,14},{4,8},{6,10},{8,20},{10,22},{12,16},{14,18},{16,28},... | collective-permute-start | bytes 405512 | tf_op jit(solution)/shard_map/ppermute | solution.py:449
  9.6 13.3 %collective-permute-start.10 = (bf16[16,4224]{1,0:T(8,128)(2,1)S(1)}, bf16[16,4224]{1,0:T(8,128)(2,1)S(1)}, u32[]{:S(2)}, u32[]{:S(2)}) collective-permute-start(bf16[16,4224]{1,0:T(8,128)(2,1)S(1)} %get-tuple-element.38), channel_id=1, source_target_pairs={{0,28},{2,30},{4,24},{6,26},{8,4},{10,6},{12,0},{14,2},{16,12},{18... | collective-permute-start | bytes 405512 | tf_op jit(solution)/shard_map/ppermute | solution.py:449
  11.8 10.4 %collective-permute-start.7 = (bf16[16,4224]{1,0:T(8,128)(2,1)S(1)}, bf16[16,4224]{1,0:T(8,128)(2,1)S(1)}, u32[]{:S(2)}, u32[]{:S(2)}) collective-permute-start(bf16[16,4224]{1,0:T(8,128)(2,1)S(1)} %get-tuple-element.35), channel_id=1, source_target_pairs={{0,8},{2,10},{4,12},{6,14},{8,16},{10,18},{12,20},{14,22},{16,24},... | collective-permute-start | bytes 405512 | tf_op jit(solution)/shard_map/ppermute | solution.py:449
  11.8 13.2 %collective-permute-start.8 = (bf16[16,4224]{1,0:T(8,128)(2,1)S(1)}, bf16[16,4224]{1,0:T(8,128)(2,1)S(1)}, u32[]{:S(2)}, u32[]{:S(2)}) collective-permute-start(bf16[16,4224]{1,0:T(8,128)(2,1)S(1)} %get-tuple-element.36), channel_id=1, source_target_pairs={{0,24},{2,26},{4,28},{6,30},{8,0},{10,2},{12,4},{14,6},{16,8},{18,... | collective-permute-start | bytes 405512 | tf_op jit(solution)/shard_map/ppermute | solution.py:449
  16.1 9.5 %collective-permute-start.6 = (bf16[16,4224]{1,0:T(8,128)(2,1)S(1)}, bf16[16,4224]{1,0:T(8,128)(2,1)S(1)}, u32[]{:S(2)}, u32[]{:S(2)}) collective-permute-start(bf16[16,4224]{1,0:T(8,128)(2,1)S(1)} %get-tuple-element.34), channel_id=1, source_target_pairs={{0,4},{2,6},{4,0},{6,2},{8,12},{10,14},{12,8},{14,10},{16,20},{18,... | collective-permute-start | bytes 405512 | tf_op jit(solution)/shard_map/ppermute | solution.py:449
  17.8 23.3 %copy-start.2 = (bf16[1,768,768]{2,1,0:T(8,128)(2,1)S(1)}, bf16[1,768,768]{2,1,0:T(8,128)(2,1)}, u32[]{:S(2)}) copy-start(bf16[1,768,768]{2,1,0:T(8,128)(2,1)} %refs_14_.1) | copy-start | bytes 3538948
  22.1 11.7 %collective-permute-start.3 = (bf16[16,4224]{1,0:T(8,128)(2,1)S(1)}, bf16[16,4224]{1,0:T(8,128)(2,1)S(1)}, u32[]{:S(2)}, u32[]{:S(2)}) collective-permute-start(bf16[16,4224]{1,0:T(8,128)(2,1)S(1)} %get-tuple-element.31), channel_id=1, source_target_pairs={{0,16},{2,18},{4,20},{6,22},{8,24},{10,26},{12,28},{14,30},{16,0},... | collective-permute-start | bytes 405512 | tf_op jit(solution)/shard_map/ppermute | solution.py:449
  22.9 13.0 %collective-permute-start.4 = (bf16[16,4224]{1,0:T(8,128)(2,1)S(1)}, bf16[16,4224]{1,0:T(8,128)(2,1)S(1)}, u32[]{:S(2)}, u32[]{:S(2)}) collective-permute-start(bf16[16,4224]{1,0:T(8,128)(2,1)S(1)} %get-tuple-element.32), channel_id=1, source_target_pairs={{0,20},{2,22},{4,16},{6,18},{8,28},{10,30},{12,24},{14,26},{16,4},... | collective-permute-start | bytes 405512 | tf_op jit(solution)/shard_map/ppermute | solution.py:449
  25.0 18.5 %collective-permute-start.14 = (bf16[32,4224]{1,0:T(8,128)(2,1)S(1)}, bf16[32,4224]{1,0:T(8,128)(2,1)S(1)}, u32[]{:S(2)}, u32[]{:S(2)}) collective-permute-start(bf16[32,4224]{1,0:T(8,128)(2,1)S(1)} %constant_dynamic-update-slice_fusion.6.refs_2_), channel_id=1, source_target_pairs={{0,1},{1,0},{2,3},{3,2},{4,5},{5,4},{6,7},{7,6},{8,9},{9,8},{10,11... | collective-permute-start | bytes 811016 | tf_op jit(solution)/shard_map/ppermute | solution.py:446
  25.6 17.9 %collective-permute-start.13 = (bf16[32,4224]{1,0:T(8,128)(2,1)S(1)}, bf16[32,4224]{1,0:T(8,128)(2,1)S(1)}, u32[]{:S(2)}, u32[]{:S(2)}) collective-permute-start(bf16[32,4224]{1,0:T(8,128)(2,1)S(1)} %constant_dynamic-update-slice_fusion.4.refs_1_), channel_id=1, source_target_pairs={{0,1},{1,0},{2,3},{3,2},{4,5},{5,4},{6,7},{7,6},{8,9},{9,8},{10,11... | collective-permute-start | bytes 811016 | tf_op jit(solution)/shard_map/ppermute | solution.py:446
  33.8 12.1 %collective-permute-start.12 = (bf16[32,4224]{1,0:T(8,128)(2,1)S(1)}, bf16[32,4224]{1,0:T(8,128)(2,1)S(1)}, u32[]{:S(2)}, u32[]{:S(2)}) collective-permute-start(bf16[32,4224]{1,0:T(8,128)(2,1)S(1)} %constant_dynamic-update-slice_fusion.2.refs_0_), channel_id=1, source_target_pairs={{0,1},{1,0},{2,3},{3,2},{4,5},{5,4},{6,7},{7,6},{8,9},{9,8},{10,11... | collective-permute-start | bytes 811016 | tf_op jit(solution)/shard_map/ppermute | solution.py:446
  35.9 15.9 %collective-permute-start.5 = (bf16[32,4224]{1,0:T(8,128)(2,1)S(1)}, bf16[32,4224]{1,0:T(8,128)(2,1)S(1)}, u32[]{:S(2)}, u32[]{:S(2)}) collective-permute-start(bf16[32,4224]{1,0:T(8,128)(2,1)S(1)} %constant_dynamic-update-slice_fusion.refs_3_), channel_id=1, source_target_pairs={{0,1},{1,0},{2,3},{3,2},{4,5},{5,4},{6,7},{7,6},{8,9},{9,8},{10,11... | collective-permute-start | bytes 811016 | tf_op jit(solution)/shard_map/ppermute | solution.py:446
  36.5 2.2 %copy-start = (bf16[1,1024,2048]{2,1,0:T(8,128)(2,1)S(1)}, bf16[1,1024,2048]{2,1,0:T(8,128)(2,1)}, u32[]{:S(2)}) copy-start(bf16[1,1024,2048]{2,1,0:T(8,128)(2,1)} %q_ref.1) | copy-start | bytes 12582916
  38.6 2.4 %copy-start.1 = (bf16[1,1024,2048]{2,1,0:T(8,128)(2,1)S(1)}, bf16[1,1024,2048]{2,1,0:T(8,128)(2,1)}, u32[]{:S(2)}) copy-start(bf16[1,1024,2048]{2,1,0:T(8,128)(2,1)} %q_ref.1) | copy-start | bytes 12582916
  39.5 19.6 %collective-permute-start.15 = (bf16[384,512]{1,0:T(8,128)(2,1)S(1)}, bf16[384,512]{1,0:T(8,128)(2,1)S(1)}, u32[]{:S(2)}, u32[]{:S(2)}) collective-permute-start(bf16[384,512]{1,0:T(8,128)(2,1)S(1)} %square.1), channel_id=1, source_target_pairs={{0,1},{1,0},{2,3},{3,2},{4,5},{5,4},{6,7},{7,6},{8,9},{9,8},{10,11... | collective-permute-start | bytes 1179656 | tf_op jit(solution)/shard_map/ppermute | solution.py:446
